TPU v7x, 128 devices: a whole 4x4x4 slice. The times are simulated.
128 devices in a mesh: depth: 4 (over y), track: 32 (over z, x, core).
Axes of the slice: x: 4, y: 4, z: 4, core: 2. Of those that a mesh axis runs over, the one named last changes fastest.
Arguments:
- slowness_cells: float32 [128, 16384], P('depth'), may hold values from 0.5 to 2
- cell_of_group: int32 [512], P('track'), may hold values from 0 to 16383
- taper: float32 [256, 9], replicated, may hold values from 0 to 0.25
- secant: float32 [256], replicated, may hold values from 1 to 3
- primary: bfloat16 [128, 16384, 256], P('depth', 'track'), may hold values from -0.3984375 to 0.3984375
- quadrature: bfloat16 [128, 16384, 256], P('depth', 'track'), may hold values from -0.3984375 to 0.3984375
- observed: float32 [128, 16384], P('depth', 'track'), may hold values from -6 to 6
Outputs:
- focused: float32 [128, 16384], P('depth', 'track')
- gradient: float32 [128, 16384], P('depth')
All inputs are finite; a program needn't handle non-finite values.
Results may differ from a plain program's by a relative error of at most 0.0003.
Values sent between devices are 32-bit elements; how exact they have to be, the bound alone decides.
A program may use at most 128 MiB of HBM per device.

v0:
```python
import jax
import jax.numpy as jnp
from jax import lax
from jax.sharding import PartitionSpec as P

OMEGA = 0.25


def with_halo(block, sides, width):
    for axis, dim in sides:
        count = lax.axis_size(axis)
        forward = [(i, i + 1) for i in range(count - 1)]
        backward = [(target, source) for source, target in forward]
        low = lax.ppermute(
            lax.slice_in_dim(block, block.shape[dim] - width, None, axis=dim), axis, forward
        )
        high = lax.ppermute(lax.slice_in_dim(block, 0, width, axis=dim), axis, backward)
        block = jnp.concatenate([low, block, high], axis=dim)
    return block


def laid_out(tiles, dim):
    tiles = jnp.moveaxis(tiles, 0, dim)
    lengths = tiles.shape
    return tiles.reshape(*lengths[:dim], lengths[dim] * lengths[dim + 1], *lengths[dim + 2 :])


def sent_to_all(value, axis):
    copies = jnp.broadcast_to(value, (lax.axis_size(axis), *value.shape))
    return lax.all_to_all(copies, axis, split_axis=0, concat_axis=0, tiled=True)


def collect(value, axis, dim):
    return laid_out(sent_to_all(value, axis), dim)


def on_device(slowness_cells, cell_of_group, taper, secant, primary, quadrature, observed):
    taps = taper.shape[1]
    reach = (taps - 1) // 2
    traces = primary.shape[1]
    nlocal = cell_of_group.shape[0]
    group = traces // nlocal
    high = lax.Precision.HIGHEST
    cells = jnp.repeat(cell_of_group, group)
    slow = jnp.take(slowness_cells, cells, axis=1)
    rimmed = with_halo(slow, (("track", 1),), reach)
    window = jnp.stack([rimmed[:, k : k + traces] for k in range(taps)], 0)
    increment = jnp.einsum("kzx,ak->zxa", window, taper, precision=high) * secant
    local = jnp.cumsum(increment, axis=0)
    mine = lax.axis_index("depth")
    totals = collect(local[-1][None], "depth", 0)
    slabs = jnp.arange(totals.shape[0])
    above = jnp.sum(jnp.where((slabs < mine)[:, None, None], totals, 0.0), axis=0)
    travel = local + above
    cosine = jnp.cos(OMEGA * travel)
    sine = jnp.sin(OMEGA * travel)
    prim = primary.astype(jnp.float32)
    quad = quadrature.astype(jnp.float32)
    focused = jnp.sum(prim * cosine + quad * sine, axis=2)
    resid = focused - observed
    time_grad = OMEGA * resid[:, :, None] * (quad * cosine - prim * sine)
    deeper = jnp.flip(jnp.cumsum(jnp.flip(time_grad, 0), axis=0), 0)
    totals_up = collect(deeper[0][None], "depth", 0)
    levels = jnp.arange(totals_up.shape[0])
    below = jnp.sum(jnp.where((levels > mine)[:, None, None], totals_up, 0.0), axis=0)
    step_grad = deeper + below
    spread = jnp.einsum("zxa,ak->kzx", step_grad * secant, taper, precision=high)
    spread = with_halo(spread, (("track", 2),), reach)
    slow_grad = jnp.zeros(slow.shape, jnp.float32)
    for k in range(taps):
        slow_grad = slow_grad + spread[k, :, 2 * reach - k : 2 * reach - k + traces]
    group_sums = jnp.sum(slow_grad.reshape(slow_grad.shape[0], nlocal, group), axis=2)
    ncells = slowness_cells.shape[1]
    all_sums, all_cells = (collect(group_sums, "track", 1), collect(cell_of_group, "track", 0))
    gradient = jax.ops.segment_sum(all_sums.T, all_cells.astype(jnp.int32), num_segments=ncells).T
    return (focused, gradient)


def solution(mesh):
    in_specs = (
        P("depth", None),
        P("track"),
        P(),
        P(),
        P("depth", "track", None),
        P("depth", "track", None),
        P("depth", "track"),
    )
    out_specs = (P("depth", "track"), P("depth", None))
    return jax.shard_map(
        on_device, mesh=mesh, in_specs=in_specs, out_specs=out_specs, check_vma=False
    )
```

profile of v0, /device:TPU:1, one launch (start us, length us, event | category | flops | bytes accessed | tf_op | source)
XLA Modules:
  0.0 339.3 jit_solution(9879088200145209578)
XLA Ops:
  0.6 0.7 broadcast_in_dim.57
  1.4 0.1 reshape.114
  1.5 6.3 %copy.31 = f32[32,16384]{0,1:T(8,128)} copy(f32[32,16384]{1,0:T(8,128)} %param.7) | data formatting | bytes 4194304 | tf_op args[0]
  7.8 4.4 %gather_fusion = f32[512,32]{1,0:T(8,128)S(1)} fusion(f32[32,16384]{0,1:T(8,128)} %copy.31, s32[1024]{0:T(1024)S(1)} %pad_clamp_fusion), kind=kCustom, calls=%fused_computation | custom fusion | bytes 133120 | tf_op jit(solution)/shard_map/jit(_take)/gather | solution.py:45
  12.2 0.1 copy.32
  12.4 4.5 %collective-permute-start = (f32[32,4]{1,0:T(8,128)S(1)}, f32[32,4]{1,0:T(8,128)S(1)}, u32[]{:S(2)}, u32[]{:S(2)}) collective-permute-start(f32[32,4]{1,0:T(8,128)S(1)} %get-tuple-element.23), channel_id=1, source_target_pairs={{0,1},{1,2},{2,3},{3,4},{4,5},{5,6},{6,7},{7,8},{8,9},{9,10},{10,1... | collective-permute-start | bytes 1544 | tf_op jit(solution)/shard_map/ppermute | solution.py:14
  16.9 1.9 collective-permute-start.1
  19.0 3.0 collective-permute-done.1
  22.0 0.2 pad_maximum_fusion.2
  22.8 1.0 stack.36
  23.8 15.9 %fusion.38 = f32[32,512,256]{2,1,0:T(8,128)} fusion(f32[9,32,512]{2,0,1:T(8,128)S(1)} %stack.36, f32[256,9]{0,1:T(8,128)S(1)} %copy-done), kind=kOutput, calls=%fused_computation.72 | convolution fusion | flops 452984832 | bytes 17376256 | tf_op jit(solution)/shard_map/kzx,ak->zxa/dot_general | solution.py:48
  39.7 6.7 %fusion.7 = f32[32,512,256]{2,1,0:T(8,128)S(1)} fusion(f32[32,512,256]{2,1,0:T(8,128)} %fusion.38, f32[256]{0:T(256)S(1)} %copy-done.5), kind=kOutput, calls=%fused_computation.14 | output fusion | flops 134217728 | bytes 33555456 | tf_op jit(solution)/shard_map/jit(cumsum)/reduce_window_sum | solution.py:49
  46.4 5.7 %copy-done.1 = f32[32,512,256]{2,1,0:T(8,128)} copy-done((f32[32,512,256]{2,1,0:T(8,128)}, f32[32,512,256]{2,1,0:T(8,128)S(1)}, u32[]{:S(2)}) %copy-start.1) | copy-done | bytes 16777240
  52.2 1.5 broadcast_in_dim.63
  53.7 4.2 %all-to-all-start = ((f32[4,1,512,256]{3,2,1,0:T(8,128)}), f32[4,1,512,256]{3,2,1,0:T(8,128)S(1)}, u32[]{:S(2)}, u32[]{:S(2)}) async-start(f32[4,1,512,256]{3,2,1,0:T(8,128)} %broadcast_in_dim.63), calls=%async_computation | async-start | bytes 4194304 | tf_op jit(solution)/shard_map/all_to_all | solution.py:30
  57.9 25.4 %all-to-all-done = f32[4,1,512,256]{3,2,1,0:T(8,128)S(1)} async-done(((f32[4,1,512,256]{3,2,1,0:T(8,128)}), f32[4,1,512,256]{3,2,1,0:T(8,128)S(1)}, u32[]{:S(2)}, u32[]{:S(2)}) %all-to-all-start) | async-done | bytes 2097184 | tf_op jit(solution)/shard_map/all_to_all | solution.py:30
  83.2 0.2 fusion.17
  83.5 67.1 %fusion.1 = f32[32,512]{1,0:T(8,128)S(1)} fusion(bf16[32,512,256]{2,1,0:T(8,128)(2,1)} %param.11, bf16[32,512,256]{2,1,0:T(8,128)(2,1)} %param.12, f32[32,512,256]{2,1,0:T(8,128)} %copy-done.1, f32[512,256]{1,0:T(8,128)S(1)} %fusion.17), kind=kLoop, calls=%fused_computation.7 | loop fusion | flops 33538048 | bytes 34144256 | tf_op jit(solution)/shard_map/reduce_sum | solution.py:59
  150.7 66.2 %fusion.3 = f32[32,512,256]{2,1,0:T(8,128)} fusion(bf16[32,512,256]{2,1,0:T(8,128)(2,1)S(1)} %bitcast.54, bf16[32,512,256]{2,1,0:T(8,128)(2,1)} %param.12, f32[32,512,256]{2,1,0:T(8,128)S(1)} %bitcast.51, f32[32,512]{1,0:T(8,128)S(1)} %subtract_multiply_fusion, f32[512,256]{1,0:T(8,128)S(1)} %fusion.17), kind=kLoop, calls=%fused_computation.9 | loop fusion | flops 33554432 | bytes 50921472 | tf_op jit(solution)/shard_map/mul | solution.py:61
  216.9 11.3 %rev.7 = f32[32,512,256]{2,1,0:T(8,128)} reverse(f32[32,512,256]{2,1,0:T(8,128)} %fusion.3), dimensions={0} | reverse | bytes 33554432 | tf_op jit(solution)/shard_map/jit(_flip)/rev | solution.py:62
  228.2 6.7 %fusion.42 = f32[32,512,256]{2,1,0:T(8,128)S(1)} fusion(f32[32,512,256]{2,1,0:T(8,128)} %rev.7), kind=kOutput, calls=%fused_computation.83 | output fusion | flops 130023424 | bytes 33554432 | tf_op jit(solution)/shard_map/jit(cumsum)/reduce_window_sum | solution.py:62
  235.0 5.7 %copy-done.2 = f32[32,512,256]{2,1,0:T(8,128)} copy-done((f32[32,512,256]{2,1,0:T(8,128)}, f32[32,512,256]{2,1,0:T(8,128)S(1)}, u32[]{:S(2)}) %copy-start.2) | copy-done | bytes 16777240
  240.7 1.5 broadcast_in_dim.68
  242.2 3.8 %all-to-all-start.2 = ((f32[4,1,512,256]{3,2,1,0:T(8,128)}), f32[4,1,512,256]{3,2,1,0:T(8,128)S(1)}, u32[]{:S(2)}, u32[]{:S(2)}) async-start(f32[4,1,512,256]{3,2,1,0:T(8,128)} %broadcast_in_dim.68), calls=%async_computation.2 | async-start | bytes 4194304 | tf_op jit(solution)/shard_map/all_to_all | solution.py:30
  246.0 11.3 %rev.8 = f32[32,512,256]{2,1,0:T(8,128)} reverse(f32[32,512,256]{2,1,0:T(8,128)} %copy-done.2), dimensions={0} | reverse | bytes 33554432 | tf_op jit(solution)/shard_map/jit(_flip)/rev | solution.py:62
  257.3 15.4 %all-to-all-done.2 = f32[4,1,512,256]{3,2,1,0:T(8,128)S(1)} async-done(((f32[4,1,512,256]{3,2,1,0:T(8,128)}), f32[4,1,512,256]{3,2,1,0:T(8,128)S(1)}, u32[]{:S(2)}, u32[]{:S(2)}) %all-to-all-start.2) | async-done | bytes 2097184 | tf_op jit(solution)/shard_map/all_to_all | solution.py:30
  272.7 0.2 fusion.16
  272.9 18.7 %fusion.18 = f32[9,32,512]{2,0,1:T(8,128)S(1)} fusion(f32[32,512,256]{2,1,0:T(8,128)} %rev.8, f32[512,256]{1,0:T(8,128)S(1)} %fusion.16, f32[256]{0:T(256)S(1)} %copy-done.5, f32[256,9]{0,1:T(8,128)S(1)} %copy-done), kind=kOutput, calls=%fused_computation.27 | convolution fusion | flops 461373440 | bytes 17901568 | tf_op jit(solution)/shard_map/zxa,ak->kzx/dot_general | solution.py:67
  291.6 0.1 fusion.40
  291.8 2.3 collective-permute-start.2
  294.1 4.1 %collective-permute-start.3 = (f32[9,32,4]{2,0,1:T(8,128)S(1)}, f32[9,32,4]{2,0,1:T(8,128)S(1)}, u32[]{:S(2)}, u32[]{:S(2)}) collective-permute-start(f32[9,32,4]{2,0,1:T(8,128)S(1)} %get-tuple-element.9), channel_id=1, source_target_pairs={{0,1},{1,2},{2,3},{3,4},{4,5},{5,6},{6,7},{7,8},{8,9},{9,10},{10,1... | collective-permute-start | bytes 13832 | tf_op jit(solution)/shard_map/ppermute | solution.py:14
  298.2 0.6 broadcast_in_dim.66
  298.8 8.3 %all-to-all-start.1 = ((s32[32,1,16]{2,1,0:T(1,128)}), s32[32,1,16]{2,1,0:T(1,128)S(1)}, u32[]{:S(2)}, u32[]{:S(2)}) async-start(s32[32,1,16]{2,1,0:T(1,128)} %broadcast_in_dim.66), calls=%async_computation.1 | async-start | bytes 32768 | tf_op jit(solution)/shard_map/all_to_all | solution.py:30
  307.1 1.5 fusion.36
  308.7 0.1 reshape.121
  308.8 0.1 reduce_sum.39
  309.0 0.8 reshape.152
  309.8 4.3 %all-to-all-done.1 = s32[32,1,16]{2,1,0:T(1,128)S(1)} async-done(((s32[32,1,16]{2,1,0:T(1,128)}), s32[32,1,16]{2,1,0:T(1,128)S(1)}, u32[]{:S(2)}, u32[]{:S(2)}) %all-to-all-start.1) | async-done | bytes 2080 | tf_op jit(solution)/shard_map/all_to_all | solution.py:30
  314.1 4.2 %all-to-all-start.3 = ((f32[32,1,512]{2,1,0:T(1,128)}), f32[32,1,512]{2,1,0:T(1,128)S(1)}, u32[]{:S(2)}, u32[]{:S(2)}) async-start(f32[32,1,512]{2,1,0:T(1,128)} %reshape.152), calls=%async_computation.3 | async-start | bytes 131072 | tf_op jit(solution)/shard_map/all_to_all | solution.py:30
  318.3 0.5 broadcast.86
  318.8 0.7 reduce.5
  319.5 0.1 reshape.132
  319.5 6.2 %all-to-all-done.3 = f32[32,1,512]{2,1,0:T(1,128)S(1)} async-done(((f32[32,1,512]{2,1,0:T(1,128)}), f32[32,1,512]{2,1,0:T(1,128)S(1)}, u32[]{:S(2)}, u32[]{:S(2)}) %all-to-all-start.3) | async-done | bytes 65568 | tf_op jit(solution)/shard_map/all_to_all | solution.py:30
  325.7 0.5 broadcast.87
  326.2 0.8 reduce.6
  327.0 0.1 reshape.153
  327.1 6.0 %scatter_custom_fusion = f32[16384,32]{1,0:T(8,128)} fusion(s32[512]{0:T(512)S(1)} %reshape.132, f32[512,32]{1,0:T(8,128)S(1)} %bitcast.55, f32[]{:T(128)} %constant.28.clone.1), kind=kCustom, calls=%fused_computation.21 | custom fusion | flops 16384 | bytes 2097156 | tf_op jit(solution)/shard_map/scatter-add | solution.py:75
  333.1 6.2 %copy.42 = f32[32,16384]{1,0:T(8,128)} copy(f32[32,16384]{0,1:T(8,128)} %bitcast.52) | data formatting | bytes 4194304
  (52 shorter events, 1.1 us)
Async XLA Ops:
  0.6 23.2 %copy-start = (f32[256,9]{0,1:T(8,128)S(1)}, f32[256,9]{0,1:T(8,128)}, u32[]{:S(2)}) copy-start(f32[256,9]{0,1:T(8,128)} %param.9) | copy-start | bytes 27652
  7.8 31.9 %copy-start.5 = (f32[256]{0:T(256)S(1)}, f32[256]{0:T(256)}, u32[]{:S(2)}) copy-start(f32[256]{0:T(256)} %param.10) | copy-start | bytes 3076
  12.4 6.5 %collective-permute-start = (f32[32,4]{1,0:T(8,128)S(1)}, f32[32,4]{1,0:T(8,128)S(1)}, u32[]{:S(2)}, u32[]{:S(2)}) collective-permute-start(f32[32,4]{1,0:T(8,128)S(1)} %get-tuple-element.23), channel_id=1, source_target_pairs={{0,1},{1,2},{2,3},{3,4},{4,5},{5,6},{6,7},{7,8},{8,9},{9,10},{10,1... | collective-permute-start | bytes 1544 | tf_op jit(solution)/shard_map/ppermute | solution.py:14
  16.9 5.1 %collective-permute-start.1 = (f32[32,4]{1,0:T(8,128)S(1)}, f32[32,4]{1,0:T(8,128)S(1)}, u32[]{:S(2)}, u32[]{:S(2)}) collective-permute-start(f32[32,4]{1,0:T(8,128)S(1)} %get-tuple-element.22), channel_id=1, source_target_pairs={{1,0},{2,1},{3,2},{4,3},{5,4},{6,5},{7,6},{8,7},{9,8},{10,9},{11,1... | collective-permute-start | bytes 1544 | tf_op jit(solution)/shard_map/ppermute | solution.py:17
  46.4 5.7 %copy-start.1 = (f32[32,512,256]{2,1,0:T(8,128)}, f32[32,512,256]{2,1,0:T(8,128)S(1)}, u32[]{:S(2)}) copy-start(f32[32,512,256]{2,1,0:T(8,128)S(1)} %fusion.7) | copy-start | bytes 50331652
  53.7 29.6 %all-to-all-start = ((f32[4,1,512,256]{3,2,1,0:T(8,128)}), f32[4,1,512,256]{3,2,1,0:T(8,128)S(1)}, u32[]{:S(2)}, u32[]{:S(2)}) async-start(f32[4,1,512,256]{3,2,1,0:T(8,128)} %broadcast_in_dim.63), calls=%async_computation | async-start | bytes 4194304 | tf_op jit(solution)/shard_map/all_to_all | solution.py:30
  83.2 67.4 %slice-start = ((s8[16777216]{0:T(1024)(128)(4,1)}), s8[4194304]{0:T(1024)(128)(4,1)S(1)}, s32[]{:S(2)}) async-start(s8[16777216]{0:T(1024)(128)(4,1)} %bitcast.50), calls=%async_computation.4 | async-start | bytes 8388608
  83.2 67.4 %slice-start.4 = ((s8[8388608]{0:T(1024)(128)(4,1)}), s8[4194304]{0:T(1024)(128)(4,1)S(1)}, s32[]{:S(2)}) async-start(s8[8388608]{0:T(1024)(128)(4,1)} %bitcast.53), calls=%async_computation.8 | async-start | bytes 8388608
  83.4 67.1 %copy-start.4 = (f32[32,512]{1,0:T(8,128)S(1)}, f32[32,512]{1,0:T(8,128)}, u32[]{:S(2)}) copy-start(f32[32,512]{1,0:T(8,128)} %param.13) | copy-start | bytes 196612
  83.5 67.2 %slice-start.1 = ((s8[16777216]{0:T(1024)(128)(4,1)}), s8[4194304]{0:T(1024)(128)(4,1)S(1)}, s32[]{:S(2)}) async-start(s8[16777216]{0:T(1024)(128)(4,1)} %bitcast.50), calls=%async_computation.5 | async-start | bytes 8388608
  83.5 67.2 %slice-start.2 = ((s8[16777216]{0:T(1024)(128)(4,1)}), s8[4194304]{0:T(1024)(128)(4,1)S(1)}, s32[]{:S(2)}) async-start(s8[16777216]{0:T(1024)(128)(4,1)} %bitcast.50), calls=%async_computation.6 | async-start | bytes 8388608
  83.5 67.2 %slice-start.3 = ((s8[16777216]{0:T(1024)(128)(4,1)}), s8[4194304]{0:T(1024)(128)(4,1)S(1)}, s32[]{:S(2)}) async-start(s8[16777216]{0:T(1024)(128)(4,1)} %bitcast.50), calls=%async_computation.7 | async-start | bytes 8388608
  83.5 67.2 %slice-start.5 = ((s8[8388608]{0:T(1024)(128)(4,1)}), s8[4194304]{0:T(1024)(128)(4,1)S(1)}, s32[]{:S(2)}) async-start(s8[8388608]{0:T(1024)(128)(4,1)} %bitcast.53), calls=%async_computation.9 | async-start | bytes 8388608
  150.6 66.3 %copy-start.3 = (f32[32,512]{1,0:T(8,128)}, f32[32,512]{1,0:T(8,128)S(1)}, u32[]{:S(2)}) copy-start(f32[32,512]{1,0:T(8,128)S(1)} %fusion.1) | copy-start | bytes 196612
  234.9 5.7 %copy-start.2 = (f32[32,512,256]{2,1,0:T(8,128)}, f32[32,512,256]{2,1,0:T(8,128)S(1)}, u32[]{:S(2)}) copy-start(f32[32,512,256]{2,1,0:T(8,128)S(1)} %fusion.42) | copy-start | bytes 50331652
  242.2 30.5 %all-to-all-start.2 = ((f32[4,1,512,256]{3,2,1,0:T(8,128)}), f32[4,1,512,256]{3,2,1,0:T(8,128)S(1)}, u32[]{:S(2)}, u32[]{:S(2)}) async-start(f32[4,1,512,256]{3,2,1,0:T(8,128)} %broadcast_in_dim.68), calls=%async_computation.2 | async-start | bytes 4194304 | tf_op jit(solution)/shard_map/all_to_all | solution.py:30
  257.3 40.9 %copy-start.6 = (s32[16]{0:T(128)S(1)}, s32[16]{0:T(128)}, u32[]{:S(2)}) copy-start(s32[16]{0:T(128)} %param.8) | copy-start | bytes 196
  291.8 15.4 %collective-permute-start.2 = (f32[9,32,4]{2,0,1:T(8,128)S(1)}, f32[9,32,4]{2,0,1:T(8,128)S(1)}, u32[]{:S(2)}, u32[]{:S(2)}) collective-permute-start(f32[9,32,4]{2,0,1:T(8,128)S(1)} %get-tuple-element.8), channel_id=1, source_target_pairs={{1,0},{2,1},{3,2},{4,3},{5,4},{6,5},{7,6},{8,7},{9,8},{10,9},{11,1... | collective-permute-start | bytes 13832 | tf_op jit(solution)/shard_map/ppermute | solution.py:17
  294.1 13.1 %collective-permute-start.3 = (f32[9,32,4]{2,0,1:T(8,128)S(1)}, f32[9,32,4]{2,0,1:T(8,128)S(1)}, u32[]{:S(2)}, u32[]{:S(2)}) collective-permute-start(f32[9,32,4]{2,0,1:T(8,128)S(1)} %get-tuple-element.9), channel_id=1, source_target_pairs={{0,1},{1,2},{2,3},{3,4},{4,5},{5,6},{6,7},{7,8},{8,9},{9,10},{10,1... | collective-permute-start | bytes 13832 | tf_op jit(solution)/shard_map/ppermute | solution.py:14
  298.8 15.3 %all-to-all-start.1 = ((s32[32,1,16]{2,1,0:T(1,128)}), s32[32,1,16]{2,1,0:T(1,128)S(1)}, u32[]{:S(2)}, u32[]{:S(2)}) async-start(s32[32,1,16]{2,1,0:T(1,128)} %broadcast_in_dim.66), calls=%async_computation.1 | async-start | bytes 32768 | tf_op jit(solution)/shard_map/all_to_all | solution.py:30
  314.1 11.6 %all-to-all-start.3 = ((f32[32,1,512]{2,1,0:T(1,128)}), f32[32,1,512]{2,1,0:T(1,128)S(1)}, u32[]{:S(2)}, u32[]{:S(2)}) async-start(f32[32,1,512]{2,1,0:T(1,128)} %reshape.152), calls=%async_computation.3 | async-start | bytes 131072 | tf_op jit(solution)/shard_map/all_to_all | solution.py:30
where the time goes:
time: 340 us; the launch traced here: 339 us
  other arithmetic  157 us (46%)
  local copies, waits for them, and re-layouts  59.6 us (18%)
  waiting for transfers between devices  54.2 us (16%)
  matrix products  34.6 us (10%)
  starting transfers between devices  33.3 us (10%)
    reduce_sum x1, other arithmetic, on_device(): focused = jnp.sum(prim * cosine + quad * sine, axis=2)  67.1 us
    mul x2, other arithmetic, on_device(): time_grad = OMEGA * resid[:, :, None] * (quad * cosine - prim * sine)  66.2 us
    all_to_all x4, waiting for transfers between devices, sent_to_all(): return lax.all_to_all(copies, axis, split_axis=0, concat_axis=0, tiled=True)  51.2 us
    unnamed x31, local copies, waits for them, and re-layouts  24.9 us
    rev x2, local copies, waits for them, and re-layouts, on_device(): deeper = jnp.flip(jnp.cumsum(jnp.flip(time_grad, 0), axis=0), 0)  22.6 us
    all_to_all x4, starting transfers between devices, sent_to_all(): return lax.all_to_all(copies, axis, split_axis=0, concat_axis=0, tiled=True)  20.5 us
    dot_general x1, matrix products, on_device(): jnp.einsum('zxa,ak->kzx', step_grad * secant, taper, precision=high)  18.7 us
    dot_general x1, matrix products, on_device(): jnp.einsum('kzx,ak->zxa', window, taper, precision=high) * secant  15.9 us
  transfers between devices with their start and end apart: 8, of which 5 were waited for; matrix products, arithmetic and copies ran while one was open for 5% of the time, Pallas kernels for 0%

commit v1 on v0

v1 whole, which is shorter than its diff:
```python
import functools
import math

import jax
import jax.numpy as jnp
from jax import lax
from jax.experimental import pallas as pl
from jax.experimental.pallas import tpu as pltpu
from jax.sharding import PartitionSpec as P

OMEGA = 0.25
GROUP = 32
LANES = 128
MESH = pl.DeviceIdType.MESH

SIN = (4.442882919178189, -7.308245695274183, 3.6063544029247794, -0.8461128632742358, 0.10982698821149484)
COS = (1.4142134964903517, -6.978850985165349, 5.739461140914948, -1.8835629076104397, 0.310698190958135)

f32 = jnp.float32
bf16 = jnp.bfloat16


def horner(coefs, u):
    value = coefs[-1] * u + coefs[-2]
    for c in coefs[-3::-1]:
        value = value * u + c
    return value


def cos_sin(turns):
    r = turns - jnp.round(turns)
    u = r * r
    s = r * horner(SIN, u)
    c = horner(COS, u)
    return 1.0 - s * s, s * c


def iota(shape, dim):
    return lax.broadcasted_iota(jnp.int32, shape, dim)


def nt(a, b):
    return lax.dot_general(a, b, (((1,), (1,)), ((), ())), preferred_element_type=f32)


def nn(a, b):
    return lax.dot_general(a, b, (((1,), (0,)), ((), ())), preferred_element_type=f32)


def split3(x):
    high = x.astype(bf16).astype(f32)
    rest = x - high
    mid = rest.astype(bf16).astype(f32)
    return jnp.concatenate([high, mid, rest - mid], axis=0).astype(bf16)


def joined3(y):
    n = y.shape[0] // 3
    return y[:n] + y[n : 2 * n] + y[2 * n :]


def one_hot(mask):
    return jnp.where(mask, 1.0, 0.0).astype(bf16)


def peer_of(k, o, nd, nt_):
    d = lax.axis_index("depth")
    t = lax.axis_index("track")
    return (lax.rem(d + k, nd), lax.rem(t + o + nt_, nt_))


def halo_copies(nd, nt_, src, tile, wide, narrow, send, recv):
    copies = []
    for i, o in enumerate((1, -1)):
        copies.append(
            pltpu.make_async_remote_copy(
                src, wide.at[i], send.at[i], recv.at[i], device_id=peer_of(0, o, nd, nt_), device_id_type=MESH
            )
        )
    for k in range(1, nd):
        for o in (-1, 0, 1):
            i = 3 * (k - 1) + o + 1
            copies.append(
                pltpu.make_async_remote_copy(
                    src.at[pl.ds(tile, 8)],
                    narrow.at[i],
                    send.at[2 + i],
                    recv.at[2 + i],
                    device_id=peer_of(k, o, nd, nt_),
                    device_id_type=MESH,
                )
            )
    return copies


def main_kernel(
    nd,
    ntr,
    nchunk,
    slow_hbm,
    cells,
    taper,
    secant,
    prim_hbm,
    quad_hbm,
    seen,
    packets,
    focused,
    slow,
    prim,
    quad,
    weights,
    spread,
    fint,
    bint,
    fedge,
    blo,
    bhi,
    halo_a,
    wide_a,
    narrow_a,
    halo_b,
    wide_b,
    narrow_b,
    mine,
    slow_sem,
    prim_sem,
    quad_sem,
    send_a,
    recv_a,
    send_b,
    recv_b,
    send_c,
    recv_c,
):
    d = lax.axis_index("depth")
    t = lax.axis_index("track")
    depth, traces, angles = prim.shape
    groups = traces // GROUP
    zc = depth // nchunk

    nblock = slow.shape[0]

    def slow_copy(i):
        lanes = pl.ds(pl.multiple_of(i * LANES, LANES), LANES)
        return pltpu.make_async_copy(slow_hbm.at[:, lanes], slow.at[i], slow_sem)

    @pl.loop(0, nblock)
    def _(i):
        slow_copy(i).start()

    def chunk_copies(i):
        rows = pl.ds(i * zc, zc)
        return (
            pltpu.make_async_copy(prim_hbm.at[rows], prim.at[rows], prim_sem.at[i]),
            pltpu.make_async_copy(quad_hbm.at[rows], quad.at[rows], quad_sem.at[i]),
        )

    @pl.loop(0, nchunk)
    def _(i):
        for copy in chunk_copies(i):
            copy.start()

    barrier = pltpu.get_barrier_semaphore()

    @pl.loop(1, ntr)
    def _(k):
        pl.semaphore_signal(barrier, inc=1, device_id=(d, lax.rem(t + k, ntr)), device_id_type=MESH)

    for k in range(1, nd):
        for o in (-1, 0, 1):
            pl.semaphore_signal(barrier, inc=1, device_id=peer_of(k, o, nd, ntr), device_id_type=MESH)

    taps = taper[...].T
    sec = secant[...] * OMEGA
    row = iota((8, angles), 0)
    nlo = jnp.where(row < 4, 4 - row, 12 - row)
    wlo = jnp.zeros((8, angles), f32)
    whi = jnp.zeros((8, angles), f32)
    for k in range(taper.shape[1]):
        tap = jnp.broadcast_to(taps[k : k + 1, :] * sec, (8, angles))
        wlo = wlo + jnp.where(k < nlo, tap, 0.0)
        whi = whi + jnp.where(k < nlo, 0.0, tap)
    weights[0] = wlo
    weights[1] = whi
    weights[2] = jnp.broadcast_to(jnp.sum(taps, axis=0, keepdims=True) * sec, (8, angles))

    nedge = groups * 8
    lane = iota((1, LANES), 1)

    e = iota((nedge, traces), 0)
    x = iota((nedge, traces), 1)
    i = lax.rem(e, 8)
    at = lax.rem((e // 8) * GROUP + jnp.where(i < 4, i, i - 8) + traces, traces)
    edge_of = one_hot(at == x)
    seen_edge = joined3(nt(split3(seen[...]), edge_of))

    @pl.loop(0, nblock)
    def _(i):
        slow_copy(i).wait()

    mine_lane = iota((depth, LANES), 1)
    own = jnp.zeros((depth, LANES), f32)
    for g in range(groups):
        c = cells[g]
        block = slow[lax.div(c, LANES)]
        column = jnp.sum(jnp.where(mine_lane == lax.rem(c, LANES), block, 0.0), axis=1, keepdims=True)
        own = jnp.where(mine_lane == g, column, own)
    zrow = iota((depth, LANES), 0)
    s = 1
    while s < depth:
        own = own + jnp.where(zrow >= s, pltpu.roll(own, s, 0), 0.0)
        s *= 2
    halo_a[...] = own

    pl.semaphore_wait(barrier, ntr - 1 + 3 * (nd - 1))
    copies = halo_copies(nd, ntr, halo_a, depth - 8, wide_a, narrow_a, send_a, recv_a)
    for copy in copies:
        copy.start()
    for copy in copies:
        copy.wait()

    def total(o, rowi, narrow, up):
        acc = jnp.zeros((1, LANES), f32)
        for k in range(1, nd):
            use = (k <= d) if up else (k > d)
            acc = acc + jnp.where(use, narrow[3 * (k - 1) + o + 1, rowi : rowi + 1, :], 0.0)
        return acc

    centre = own + total(0, 7, narrow_a, True)
    left = jnp.where(t > 0, wide_a[0] + total(1, 7, narrow_a, True), 0.0)
    right = jnp.where(t < ntr - 1, wide_a[1] + total(-1, 7, narrow_a, True), 0.0)
    summed = jnp.where(mine_lane < groups, centre, 0.0)
    summed = jnp.where(mine_lane == groups, pltpu.roll(left, 1, 1), summed)
    summed = jnp.where(mine_lane == groups + 1, pltpu.roll(right, groups + 1, 1), summed)
    halo_a[...] = summed * (1.0 / (2.0 * math.pi))

    nrow = spread.shape[1]
    diagonal = iota((nrow, LANES), 0) == iota((nrow, LANES), 1)

    @pl.loop(0, depth, unroll=4)
    def _(z):
        line = jnp.broadcast_to(halo_a[pl.ds(z, 1), :], (nrow, LANES))
        spread[z] = jnp.broadcast_to(
            jnp.sum(jnp.where(diagonal, line, 0.0), axis=1, keepdims=True), (nrow, LANES)
        )

    sub = iota((8, angles), 0)
    upper = sub < 4
    sub128 = iota((8, LANES), 0)
    lane128 = iota((8, LANES), 1)
    place = lax.rem(lane128, 8) == sub128
    half = 256
    own_group = sub == iota((8, half), 1) // GROUP

    def each_depth(z):
        for h in range(traces // half):
            first = h * half // GROUP
            c8 = spread[z, first : first + 8, :]
            w = weights[2]
            c, s = cos_sin(w * jnp.concatenate([c8] * (angles // LANES), axis=1))
            wc = w * c
            ws = w * s

            def pair(v):
                return [v, v - v.astype(bf16).astype(f32)]

            lhs_p = jnp.concatenate(pair(c) + pair(-ws), axis=0).astype(bf16)
            lhs_q = jnp.concatenate(pair(s) + pair(wc), axis=0).astype(bf16)
            rows = pl.ds(h * half, half)
            out = nt(lhs_p, prim[z, rows, :]) + nt(lhs_q, quad[z, rows, :])
            fsum = jnp.where(own_group, out[0:8] + out[8:16], 0.0)
            bsum = jnp.where(own_group, out[16:24] + out[24:32], 0.0)
            fint[pl.ds(z, 1), rows] = jnp.sum(fsum, axis=0, keepdims=True)
            bint[pl.ds(z, 1), rows] = jnp.sum(bsum, axis=0, keepdims=True)
        acc_f = jnp.zeros((8, LANES), f32)
        acc_lo = jnp.zeros((8, LANES), f32)
        acc_hi = jnp.zeros((8, LANES), f32)
        for b in range(groups):

            def splat(r):
                return jnp.broadcast_to(spread[z, r : r + 1, :], (8, LANES))

            if b == 0:
                clo = jnp.where(sub128 < 4, splat(groups), splat(groups - 1))
                chi = jnp.where(sub128 < 4, splat(0), splat(groups + 1))
            else:
                clo = splat(b - 1)
                chi = splat(b)
            clo = jnp.concatenate([clo] * (angles // LANES), axis=1)
            chi = jnp.concatenate([chi] * (angles // LANES), axis=1)

            def edge_rows(ref):
                behind = ref[z, GROUP * b : GROUP * b + 8, :].astype(f32)
                stop = GROUP * b if b else traces
                before = ref[z, stop - 8 : stop, :].astype(f32)
                return jnp.where(upper, behind, before)

            pe = edge_rows(prim)
            qe = edge_rows(quad)
            wlo = weights[0]
            whi = weights[1]
            c, s = cos_sin(wlo * clo + whi * chi)
            g = qe * c - pe * s
            here = lane128 // 8 == b
            acc_f = jnp.where(here, jnp.sum(pe * c + qe * s, axis=1, keepdims=True), acc_f)
            acc_lo = jnp.where(here, jnp.sum(g * wlo, axis=1, keepdims=True), acc_lo)
            acc_hi = jnp.where(here, jnp.sum(g * whi, axis=1, keepdims=True), acc_hi)
        for acc, ref in ((acc_f, fedge), (acc_lo, blo), (acc_hi, bhi)):
            ref[pl.ds(z, 1), :] = jnp.sum(jnp.where(place, acc, 0.0), axis=0, keepdims=True)

    @pl.loop(0, nchunk)
    def _(i):
        for copy in chunk_copies(i):
            copy.wait()

        @pl.loop(0, zc)
        def _(j):
            each_depth(i * zc + j)

    xoff = lax.rem(iota((depth, traces), 1), GROUP)
    inner = (xoff >= 4) & (xoff < GROUP - 4)
    term = jnp.where(inner, (fint[...] - seen[...]) * bint[...], 0.0)
    resid = fedge[...] - seen_edge
    xg = iota((traces, LANES), 0) // GROUP
    to_own = one_hot(xg == iota((traces, LANES), 1))
    eb = iota((nedge, LANES), 0)
    el = iota((nedge, LANES), 1)
    bi = eb // 8
    upper_row = lax.rem(eb, 8) < 4
    lo_target = jnp.where(bi > 0, bi - 1, jnp.where(upper_row, groups, groups - 1))
    hi_target = jnp.where((bi > 0) | upper_row, bi, groups + 1)
    sums = joined3(nn(split3(term), to_own))
    sums = sums + joined3(nn(split3(resid * blo[...]), one_hot(lo_target == el)))
    sums = sums + joined3(nn(split3(resid * bhi[...]), one_hot(hi_target == el)))
    s = 1
    while s < depth:
        sums = sums + jnp.where(zrow < depth - s, pltpu.roll(sums, depth - s, 0), 0.0)
        s *= 2
    halo_b[...] = sums

    copies = halo_copies(nd, ntr, halo_b, 0, wide_b, narrow_b, send_b, recv_b)
    for copy in copies:
        copy.start()
    full = jnp.where(inner, fint[...], joined3(nn(split3(fedge[...]), edge_of)))
    focused[...] = full
    cell_lanes = jnp.zeros((8, LANES), f32)
    for g in range(groups):
        cell_lanes = jnp.where(lane128 == 4 * groups + g, cells[g].astype(f32), cell_lanes)
    for copy in copies:
        copy.wait()

    centre = sums + total(0, 0, narrow_b, False)
    left = jnp.where(t > 0, wide_b[0] + total(1, 0, narrow_b, False), 0.0)
    right = jnp.where(t < ntr - 1, wide_b[1] + total(-1, 0, narrow_b, False), 0.0)
    grads = jnp.where(mine_lane < groups, centre, 0.0)
    grads = grads + jnp.where(mine_lane == 0, pltpu.roll(left, LANES - groups - 1, 1), 0.0)
    grads = grads + jnp.where(mine_lane == groups - 1, pltpu.roll(right, LANES - 1, 1), 0.0)
    packet = cell_lanes
    for q in range(depth // 8):
        block = grads[8 * q : 8 * q + 8]
        packet = packet + (pltpu.roll(block, groups * q, 1) if q else block)
    per = LANES // groups
    packet = pltpu.roll(packet, groups * lax.rem(t, per), 1)
    mine[...] = packet
    packets[t] = packet

    def packet_copy(k):
        return pltpu.make_async_remote_copy(
            mine,
            packets.at[t],
            send_c.at[k],
            recv_c.at[k],
            device_id=(d, lax.rem(t + k, ntr)),
            device_id_type=MESH,
        )

    def packet_arrival(k):
        return pltpu.make_async_remote_copy(
            mine,
            packets.at[lax.rem(t + ntr - k, ntr)],
            send_c.at[k],
            recv_c.at[k],
            device_id=(d, lax.rem(t + k, ntr)),
            device_id_type=MESH,
        )

    @pl.loop(1, ntr)
    def _(k):
        packet_copy(k).start()

    @pl.loop(1, ntr)
    def _(k):
        packet_copy(k).wait_send()
        packet_arrival(k).wait_recv()


WIDE = 256
STEPS = 8


def scatter_kernel(groups, packets, focused, grad, image, ghigh, glow, block_of, place):
    ntr = packets.shape[0]
    per = LANES // groups
    depth = grad.shape[0]
    total = ntr * groups
    step = pl.program_id(0)

    @pl.when(step == 0)
    def _():
        image[...] = focused[...]
        chunk = iota((8, LANES), 1) // groups
        for col in range(ntr // per):
            parts = []
            for q in range(depth // 8 + 1):
                acc = jnp.zeros((8, LANES), f32)
                for j in range(per):
                    acc = jnp.where(chunk == (q + j) % per, packets[col * per + j], acc)
                parts.append(pltpu.roll(acc, LANES - groups * q, 1) if q else acc)
            at = pl.ds(col * LANES, LANES)
            g = jnp.concatenate(parts[:-1], axis=0)
            high = g.astype(bf16)
            ghigh[:, at] = high
            glow[:, at] = (g - high.astype(f32)).astype(bf16)
            cell = parts[-1][0:1]
            block = jnp.floor(cell * (1.0 / WIDE))
            block_of[:, at] = jnp.broadcast_to(block, (depth, LANES)).astype(bf16)
            inside = cell - block * WIDE
            place[:, at] = one_hot(iota((WIDE, LANES), 0).astype(f32) == inside)

    nblock = grad.shape[1] // WIDE
    highs = []
    lows = []
    for j in range(nblock):
        mask = block_of[...] == (step * nblock + j).astype(bf16)
        highs.append(jnp.where(mask, ghigh[...], jnp.zeros((), bf16)))
        lows.append(jnp.where(mask, glow[...], jnp.zeros((), bf16)))
    out = nt(jnp.concatenate(highs, axis=0), place[...]) + nt(jnp.concatenate(lows, axis=0), place[...])
    for j in range(nblock):
        grad[:, j * WIDE : (j + 1) * WIDE] = out[depth * j : depth * (j + 1)]


def on_device(nd, ntr, slowness_cells, cell_of_group, taper, secant, primary, quadrature, observed):
    depth, traces, angles = primary.shape
    ncell = slowness_cells.shape[1]
    groups = cell_of_group.shape[0]
    nchunk = 8
    vmem = pl.BlockSpec(memory_space=pltpu.VMEM)
    anywhere = pl.BlockSpec(memory_space=pltpu.HBM)
    nhalo = 2 + 3 * (nd - 1)
    dma = pltpu.SemaphoreType.DMA
    packets, focused = pl.pallas_call(
        functools.partial(main_kernel, nd, ntr, nchunk),
        out_shape=(
            jax.ShapeDtypeStruct((ntr, 8, LANES), f32),
            jax.ShapeDtypeStruct((depth, traces), f32),
        ),
        in_specs=[anywhere, pl.BlockSpec(memory_space=pltpu.SMEM), vmem, vmem, anywhere, anywhere, vmem],
        out_specs=(vmem, vmem),
        scratch_shapes=[
            pltpu.VMEM((ncell // LANES, depth, LANES), f32),
            pltpu.VMEM((depth, traces, angles), bf16),
            pltpu.VMEM((depth, traces, angles), bf16),
            pltpu.VMEM((3, 8, angles), f32),
            pltpu.VMEM((depth, 24, LANES), f32),
            pltpu.VMEM((depth, traces), f32),
            pltpu.VMEM((depth, traces), f32),
            pltpu.VMEM((depth, LANES), f32),
            pltpu.VMEM((depth, LANES), f32),
            pltpu.VMEM((depth, LANES), f32),
            pltpu.VMEM((depth, LANES), f32),
            pltpu.VMEM((2, depth, LANES), f32),
            pltpu.VMEM((3 * (nd - 1), 8, LANES), f32),
            pltpu.VMEM((depth, LANES), f32),
            pltpu.VMEM((2, depth, LANES), f32),
            pltpu.VMEM((3 * (nd - 1), 8, LANES), f32),
            pltpu.VMEM((8, LANES), f32),
            dma,
            dma((nchunk,)),
            dma((nchunk,)),
            dma((nhalo,)),
            dma((nhalo,)),
            dma((nhalo,)),
            dma((nhalo,)),
            dma((ntr,)),
            dma((ntr,)),
        ],
        compiler_params=pltpu.CompilerParams(
            collective_id=0, has_side_effects=True, vmem_limit_bytes=63 * 1024 * 1024
        ),
        name="radargram",
    )(slowness_cells, cell_of_group, taper, secant.reshape(1, angles), primary, quadrature, observed)

    wide = ncell // STEPS
    gradient, image = pl.pallas_call(
        functools.partial(scatter_kernel, groups),
        out_shape=(
            jax.ShapeDtypeStruct((depth, ncell), f32),
            jax.ShapeDtypeStruct((depth, traces), f32),
        ),
        grid=(STEPS,),
        in_specs=[
            pl.BlockSpec((ntr, 8, LANES), lambda i: (0, 0, 0)),
            pl.BlockSpec((depth, traces), lambda i: (0, 0)),
        ],
        out_specs=(
            pl.BlockSpec((depth, wide), lambda i: (0, i)),
            pl.BlockSpec((depth, traces), lambda i: (0, 0)),
        ),
        scratch_shapes=[
            pltpu.VMEM((depth, ntr * groups), bf16),
            pltpu.VMEM((depth, ntr * groups), bf16),
            pltpu.VMEM((depth, ntr * groups), bf16),
            pltpu.VMEM((WIDE, ntr * groups), bf16),
        ],
        compiler_params=pltpu.CompilerParams(dimension_semantics=("arbitrary",)),
        name="scatter",
    )(packets, focused)
    return image, gradient


def solution(mesh):
    in_specs = (
        P("depth", None),
        P("track"),
        P(),
        P(),
        P("depth", "track", None),
        P("depth", "track", None),
        P("depth", "track"),
    )
    out_specs = (P("depth", "track"), P("depth", None))
    nd = mesh.shape["depth"]
    ntr = mesh.shape["track"]
    return jax.shard_map(
        functools.partial(on_device, nd, ntr), mesh=mesh, in_specs=in_specs, out_specs=out_specs, check_vma=False
    )
```

time: 340 us -> 47.3 us (0.14)
  other arithmetic: 157 us -> 0 us
  local copies, waits for them, and re-layouts: 59.6 us -> 1.48 us
  waiting for transfers between devices: 54.2 us -> 0 us
  Pallas kernels: 0 us -> 45 us
  matrix products: 34.6 us -> 0 us
  starting transfers between devices: 33.3 us -> 0 us
    reduce_sum x4 -> x0, other arithmetic: 67.6 us -> none  [the longest x1 67.1 us: on_device(): focused = jnp.sum(prim * cosine + quad * sine, axis=2)]
    mul x2 -> x0, other arithmetic: 66.2 us -> none  [on_device(): time_grad = OMEGA * resid[:, :, None] * (quad * cosine - prim * sine)]
    all_to_all x4 -> x0, waiting for transfers between devices: 51.2 us -> none  [sent_to_all(): return lax.all_to_all(copies, axis, split_axis=0, concat_axis=0, tiled=True)]
    pallas_call x0 -> x2, Pallas kernels: none -> 45 us  [the longest x1 39.4 us: on_device(): pl.pallas_call(functools.partial(main_kernel, nd, ntr, nchunk), out_shape...]
    dot_general x2 -> x0, matrix products: 34.6 us -> none  [the longest x1 18.7 us: on_device(): jnp.einsum('zxa,ak->kzx', step_grad * secant, taper, precision=high)]
    unnamed x31 -> x1, local copies, waits for them, and re-layouts: 24.9 us -> 1.48 us
    rev x2 -> x0, local copies, waits for them, and re-layouts: 22.6 us -> none  [on_device(): deeper = jnp.flip(jnp.cumsum(jnp.flip(time_grad, 0), axis=0), 0)]
    all_to_all x4 -> x0, starting transfers between devices: 20.5 us -> none  [sent_to_all(): return lax.all_to_all(copies, axis, split_axis=0, concat_axis=0, tiled=True)]
  transfers between devices with their start and end apart: 8 -> 0, of which waited for: 5 -> 0; matrix products, arithmetic and copies ran while one was open for 5% -> 0% of each run, Pallas kernels for 0% -> 0%
where the time goes in v1:
time: 47.3 us; the launch traced here: 47.1 us
  Pallas kernels  45 us (95%)
  local copies, waits for them, and re-layouts  1.48 us (3%)
  between operations  0.64 us (1%)
    pallas_call x1, Pallas kernels, on_device(): pl.pallas_call(functools.partial(main_kernel, nd, ntr, nchunk), out_shape...  39.4 us
    pallas_call x1, Pallas kernels, on_device(): pl.pallas_call(functools.partial(scatter_kernel, groups), out_shape=(jax....  5.59 us
    unnamed x1, local copies, waits for them, and re-layouts  1.48 us

profile of v1, /device:TPU:1, one launch (start us, length us, event | category | flops | bytes accessed | tf_op | source)
XLA Modules:
  0.0 47.1 jit_solution(17031070089351306888)
XLA Ops:
  0.6 1.5 %copy.9.taper = f32[256,9]{1,0:T(8,128)} copy(f32[256,9]{0,1:T(8,128)} %param.9) | data formatting | bytes 18432 | tf_op args[2]
  2.1 39.4 %radargram.1 = (f32[32,8,128]{2,1,0:T(8,128)}, f32[32,512]{1,0:T(8,128)}) custom-call(f32[32,16384]{1,0:T(8,128)} %slow_hbm.1, s32[16]{0:T(128)} %cells.1, f32[256,9]{1,0:T(8,128)} %copy.9.taper, f32[1,256]{1,0:T(1,128)} %bitcast.1, bf16[32,512,256]{2,1,0:T(8,128)(2,1)} %prim_hbm.1, bf16[32,512,256]{2,1,0:T(8,128)(2,1)} %quad_hbm.1, f32[32,512]{1,0:T(8,128)} %seen.1), custom_call_target="tpu_custom_call" | custom-call | tf_op jit(solution)/shard_map/radargram/pallas_call | solution.py:452
  41.5 5.6 %scatter.1 = (f32[32,16384]{1,0:T(8,128)}, f32[32,512]{1,0:T(8,128)}) custom-call(f32[32,8,128]{2,1,0:T(8,128)} %get-tuple-element.6.packets, f32[32,512]{1,0:T(8,128)} %get-tuple-element.7.focused), custom_call_target="tpu_custom_call" | custom-call | tf_op jit(solution)/shard_map/scatter/pallas_call | solution.py:495

commit v2 on v1

v2 whole, which is shorter than its diff:
```python
import functools
import math

import jax
import jax.numpy as jnp
from jax import lax
from jax.experimental import pallas as pl
from jax.experimental.pallas import tpu as pltpu
from jax.sharding import PartitionSpec as P

OMEGA = 0.25
GROUP = 32
LANES = 128
MESH = pl.DeviceIdType.MESH

SIN = (4.442882919178189, -7.308245695274183, 3.6063544029247794, -0.8461128632742358, 0.10982698821149484)
COS = (1.4142134964903517, -6.978850985165349, 5.739461140914948, -1.8835629076104397, 0.310698190958135)

f32 = jnp.float32
bf16 = jnp.bfloat16


def horner(coefs, u):
    value = coefs[-1] * u + coefs[-2]
    for c in coefs[-3::-1]:
        value = value * u + c
    return value


def cos_sin(turns):
    r = turns - jnp.round(turns)
    u = r * r
    s = r * horner(SIN, u)
    c = horner(COS, u)
    return 1.0 - s * s, s * c


def iota(shape, dim):
    return lax.broadcasted_iota(jnp.int32, shape, dim)


def nt(a, b):
    return lax.dot_general(a, b, (((1,), (1,)), ((), ())), preferred_element_type=f32)


def nn(a, b):
    return lax.dot_general(a, b, (((1,), (0,)), ((), ())), preferred_element_type=f32)


def split3(x):
    high = x.astype(bf16).astype(f32)
    rest = x - high
    mid = rest.astype(bf16).astype(f32)
    return jnp.concatenate([high, mid, rest - mid], axis=0).astype(bf16)


def joined3(y):
    n = y.shape[0] // 3
    return y[:n] + y[n : 2 * n] + y[2 * n :]


def one_hot(mask):
    return jnp.where(mask, 1.0, 0.0).astype(bf16)


def peer_of(k, o, nd, nt_):
    d = lax.axis_index("depth")
    t = lax.axis_index("track")
    return (lax.rem(d + k, nd), lax.rem(t + o + nt_, nt_))


def near_copies(nd, nt_, src, tile, into, send, recv):
    return [
        pltpu.make_async_remote_copy(
            src.at[pl.ds(tile, 8)],
            into.at[k - 1],
            send.at[k - 1],
            recv.at[k - 1],
            device_id=peer_of(k, 0, nd, nt_),
            device_id_type=MESH,
        )
        for k in range(1, nd)
    ]


def side_copies(nd, nt_, src, tile, wide, narrow, send, recv):
    copies = []
    for i, o in enumerate((1, -1)):
        copies.append(
            pltpu.make_async_remote_copy(
                src, wide.at[i], send.at[i], recv.at[i], device_id=peer_of(0, o, nd, nt_), device_id_type=MESH
            )
        )
    for k in range(1, nd):
        for i, o in enumerate((1, -1)):
            at = 2 * (k - 1) + i
            copies.append(
                pltpu.make_async_remote_copy(
                    src.at[pl.ds(tile, 8)],
                    narrow.at[at],
                    send.at[2 + at],
                    recv.at[2 + at],
                    device_id=peer_of(k, o, nd, nt_),
                    device_id_type=MESH,
                )
            )
    return copies


WIDE = 256
PER_STEP = 8


def main_kernel(
    nd,
    ntr,
    nchunk,
    slow_hbm,
    cells_hbm,
    taper_hbm,
    secant_hbm,
    prim_hbm,
    quad_hbm,
    seen_hbm,
    grad,
    focused,
    cells,
    taper,
    secant,
    seen,
    slow,
    prim,
    quad,
    weights,
    line,
    spread,
    fint,
    bint,
    fedge,
    blo,
    bhi,
    fside,
    loside,
    hiside,
    edge_of,
    to_own,
    to_lo,
    to_hi,
    halo_a,
    near_a,
    wide_a,
    narrow_a,
    halo_b,
    wide_b,
    narrow_b,
    halo_c,
    near_c,
    mine,
    packets,
    below_mine,
    belows,
    ghigh,
    glow,
    block_of,
    place_of,
    rows_of,
    small_sem,
    slow_sem,
    prim_sem,
    quad_sem,
    send_a,
    recv_a,
    send_as,
    recv_as,
    send_b,
    recv_b,
    send_c,
    recv_c,
    send_p,
    recv_p,
    send_q,
    recv_q,
):
    d = lax.axis_index("depth")
    t = lax.axis_index("track")
    depth, traces, angles = prim.shape
    groups = traces // GROUP
    zc = depth // nchunk
    per = LANES // groups

    barrier = pltpu.get_barrier_semaphore()
    slow_copy = pltpu.make_async_copy(slow_hbm, slow, slow_sem)
    small = [
        pltpu.make_async_copy(cells_hbm, cells, small_sem.at[0]),
        pltpu.make_async_copy(taper_hbm, taper, small_sem.at[1]),
        pltpu.make_async_copy(secant_hbm, secant, small_sem.at[2]),
        pltpu.make_async_copy(seen_hbm, seen, small_sem.at[3]),
    ]
    small[0].start()
    slow_copy.start()

    @pl.loop(1, ntr)
    def _(k):
        pl.semaphore_signal(barrier, inc=1, device_id=(d, lax.rem(t + k, ntr)), device_id_type=MESH)

    for k in range(1, nd):
        for o in (-1, 0, 1):
            pl.semaphore_signal(barrier, inc=1, device_id=peer_of(k, o, nd, ntr), device_id_type=MESH)
    for copy in small[1:]:
        copy.start()

    def chunk_copies(i):
        rows = pl.ds(i * zc, zc)
        return (
            pltpu.make_async_copy(prim_hbm.at[rows], prim.at[rows], prim_sem.at[i]),
            pltpu.make_async_copy(quad_hbm.at[rows], quad.at[rows], quad_sem.at[i]),
        )

    mine_lane = iota((depth, LANES), 1)
    zrow = iota((depth, LANES), 0)
    small[0].wait()
    slow_copy.wait()

    @pl.loop(0, nchunk)
    def _(i):
        for copy in chunk_copies(i):
            copy.start()

    own = jnp.zeros((depth, LANES), f32)
    for g in range(groups):
        c = cells[g]
        block = slow[:, lax.div(c, LANES)].reshape(depth, LANES)
        column = jnp.sum(jnp.where(mine_lane == lax.rem(c, LANES), block, 0.0), axis=1, keepdims=True)
        own = jnp.where(mine_lane == g, column, own)
    s = 1
    while s < depth:
        own = own + jnp.where(zrow >= s, pltpu.roll(own, s, 0), 0.0)
        s *= 2
    halo_a[...] = own

    pl.semaphore_wait(barrier, ntr - 1 + 3 * (nd - 1))
    near = near_copies(nd, ntr, halo_a, depth - 8, near_a, send_a, recv_a)
    side_a = side_copies(nd, ntr, halo_a, depth - 8, wide_a, narrow_a, send_as, recv_as)
    for copy in near + side_a:
        copy.start()

    for copy in small[1:]:
        copy.wait()
    taps = taper[...]
    sec = secant[...] * OMEGA
    row = iota((8, angles), 0)
    nlo = jnp.where(row < 4, 4 - row, 12 - row)
    wlo = jnp.zeros((8, angles), f32)
    whi = jnp.zeros((8, angles), f32)
    for k in range(taper.shape[0]):
        tap = jnp.broadcast_to(taps[k : k + 1, :] * sec, (8, angles))
        wlo = wlo + jnp.where(k < nlo, tap, 0.0)
        whi = whi + jnp.where(k < nlo, 0.0, tap)
    weights[0] = wlo
    weights[1] = whi
    weights[2] = jnp.broadcast_to(jnp.sum(taps, axis=0, keepdims=True) * sec, (8, angles))

    nedge = groups * 8
    e = iota((nedge, traces), 0)
    x = iota((nedge, traces), 1)
    i = lax.rem(e, 8)
    at = lax.rem(lax.div(e, 8) * GROUP + jnp.where(i < 4, i, i - 8) + traces, traces)
    edge_of[...] = one_hot(at == x)
    to_own[...] = one_hot(lax.div(iota((traces, LANES), 0), GROUP) == iota((traces, LANES), 1))
    eb = iota((nedge, LANES), 0)
    el = iota((nedge, LANES), 1)
    bi = lax.div(eb, 8)
    behind_row = lax.rem(eb, 8) < 4
    to_lo[...] = one_hot(jnp.where(bi > 0, bi - 1, jnp.where(behind_row, groups, groups - 1)) == el)
    to_hi[...] = one_hot(jnp.where((bi > 0) | behind_row, bi, groups + 1) == el)
    seen_edge = joined3(nt(split3(seen[...]), edge_of[...]))

    for copy in near:
        copy.wait()

    def near_total(into, rowi, up):
        acc = jnp.zeros((1, LANES), f32)
        for k in range(1, nd):
            acc = acc + jnp.where((k <= d) if up else (k > d), into[k - 1, rowi : rowi + 1, :], 0.0)
        return acc

    def side_total(i, rowi, narrow, up):
        acc = jnp.zeros((1, LANES), f32)
        for k in range(1, nd):
            use = (k <= d) if up else (k > d)
            acc = acc + jnp.where(use, narrow[2 * (k - 1) + i, rowi : rowi + 1, :], 0.0)
        return acc

    turn = 1.0 / (2.0 * math.pi)
    line[...] = (own + near_total(near_a, 7, True)) * turn

    def spread_rows(first, count):
        diagonal = iota((count, LANES), 0) + first == iota((count, LANES), 1)

        @pl.loop(0, depth, unroll=8)
        def _(z):
            lines = jnp.broadcast_to(line[pl.ds(z, 1), :], (count, LANES))
            spread[z, first : first + count, :] = jnp.broadcast_to(
                jnp.sum(jnp.where(diagonal, lines, 0.0), axis=1, keepdims=True), (count, LANES)
            )

    spread_rows(0, groups)

    sub = iota((8, angles), 0)
    upper = sub < 4
    sub128 = iota((8, LANES), 0)
    lane128 = iota((8, LANES), 1)
    place = lax.rem(lane128, 8) == sub128
    half = 256
    own_group = sub == lax.div(iota((8, half), 1), GROUP)

    def splat(z, r):
        return jnp.broadcast_to(spread[z, r : r + 1, :], (8, LANES))

    def edge_sums(z, b, clo, chi):
        clo = jnp.concatenate([clo] * (angles // LANES), axis=1)
        chi = jnp.concatenate([chi] * (angles // LANES), axis=1)

        def edge_rows(ref):
            behind = ref[z, GROUP * b : GROUP * b + 8, :].astype(f32)
            stop = GROUP * b if b else traces
            before = ref[z, stop - 8 : stop, :].astype(f32)
            return jnp.where(upper, behind, before)

        pe = edge_rows(prim)
        qe = edge_rows(quad)
        wlo = weights[0]
        whi = weights[1]
        c, s = cos_sin(wlo * clo + whi * chi)
        g = qe * c - pe * s
        return [jnp.sum(v, axis=1, keepdims=True) for v in (pe * c + qe * s, g * wlo, g * whi)]

    def each_depth(z):
        for h in range(traces // half):
            first = h * half // GROUP
            c8 = spread[z, first : first + 8, :]
            w = weights[2]
            c, s = cos_sin(w * jnp.concatenate([c8] * (angles // LANES), axis=1))
            wc = w * c
            ws = w * s

            def pair(v):
                return [v, v - v.astype(bf16).astype(f32)]

            lhs_p = jnp.concatenate(pair(c) + pair(-ws), axis=0).astype(bf16)
            lhs_q = jnp.concatenate(pair(s) + pair(wc), axis=0).astype(bf16)
            rows = pl.ds(h * half, half)
            out = nt(lhs_p, prim[z, rows, :]) + nt(lhs_q, quad[z, rows, :])
            fsum = jnp.where(own_group, out[0:8] + out[8:16], 0.0)
            bsum = jnp.where(own_group, out[16:24] + out[24:32], 0.0)
            fint[pl.ds(z, 1), rows] = jnp.sum(fsum, axis=0, keepdims=True)
            bint[pl.ds(z, 1), rows] = jnp.sum(bsum, axis=0, keepdims=True)
        accs = [jnp.zeros((8, LANES), f32)] * 3
        for b in range(1, groups):
            here = lax.div(lane128, 8) == b
            found = edge_sums(z, b, splat(z, b - 1), splat(z, b))
            accs = [jnp.where(here, v, acc) for v, acc in zip(found, accs)]
        for acc, ref in zip(accs, (fedge, blo, bhi)):
            ref[pl.ds(z, 1), :] = jnp.sum(jnp.where(place, acc, 0.0), axis=0, keepdims=True)

    def outer_edge(z):
        clo = jnp.where(sub128 < 4, splat(z, groups), splat(z, groups - 1))
        chi = jnp.where(sub128 < 4, splat(z, 0), splat(z, groups + 1))
        found = edge_sums(z, 0, clo, chi)
        for v, ref in zip(found, (fside, loside, hiside)):
            picked = jnp.where(place & (lane128 < 8), v, 0.0)
            ref[pl.ds(z, 1), :] = jnp.sum(picked, axis=0, keepdims=True)

    @pl.loop(0, nchunk // 2)
    def _(i):
        for copy in chunk_copies(i):
            copy.wait()

        @pl.loop(0, zc, unroll=UNROLL)
        def _(j):
            each_depth(i * zc + j)

    for i in range(nchunk // 2, nchunk):
        for copy in chunk_copies(i):
            copy.wait()

    for copy in side_a:
        copy.wait()
    left = jnp.where(t > 0, wide_a[0] + side_total(0, 7, narrow_a, True), 0.0) * turn
    right = jnp.where(t < ntr - 1, wide_a[1] + side_total(1, 7, narrow_a, True), 0.0) * turn
    outer = jnp.where(mine_lane == groups, pltpu.roll(left, 1, 1), 0.0)
    line[...] = jnp.where(mine_lane == groups + 1, pltpu.roll(right, groups + 1, 1), outer)
    spread_rows(groups, 8)

    @pl.loop(0, depth, unroll=8)
    def _(z):
        outer_edge(z)

    def suffix(v):
        s = 1
        while s < depth:
            v = v + jnp.where(zrow < depth - s, pltpu.roll(v, depth - s, 0), 0.0)
            s *= 2
        return v

    resid = fside[...] - seen_edge
    to_left = jnp.sum(jnp.where(mine_lane < 4, resid * loside[...], 0.0), axis=1, keepdims=True)
    to_right = jnp.sum(
        jnp.where((mine_lane >= 4) & (mine_lane < 8), resid * hiside[...], 0.0), axis=1, keepdims=True
    )
    halo_b[...] = suffix(
        jnp.where(mine_lane == groups, to_left, jnp.where(mine_lane == groups + 1, to_right, 0.0))
    )
    side_b = side_copies(nd, ntr, halo_b, 0, wide_b, narrow_b, send_b, recv_b)
    for copy in side_b:
        copy.start()

    @pl.loop(depth // 2, depth, unroll=UNROLL)
    def _(z):
        each_depth(z)

    xoff = lax.rem(iota((depth, traces), 1), GROUP)
    inner = (xoff >= 4) & (xoff < GROUP - 4)
    term = jnp.where(inner, (fint[...] - seen[...]) * bint[...], 0.0)
    edge = fedge[...] + fside[...]
    resid = edge - seen_edge
    sums = joined3(nn(split3(term), to_own[...]))
    sums = sums + joined3(nn(split3(resid * (blo[...] + loside[...])), to_lo[...]))
    sums = sums + joined3(nn(split3(resid * (bhi[...] + hiside[...])), to_hi[...]))
    sums = suffix(sums)
    halo_c[...] = sums
    near = near_copies(nd, ntr, halo_c, 0, near_c, send_c, recv_c)
    for copy in near:
        copy.start()

    for copy in side_b:
        copy.wait()
    left = jnp.where(t > 0, wide_b[0] + side_total(0, 0, narrow_b, False), 0.0)
    right = jnp.where(t < ntr - 1, wide_b[1] + side_total(1, 0, narrow_b, False), 0.0)
    grads = jnp.where(mine_lane < groups, sums, 0.0)
    grads = grads + jnp.where(mine_lane == 0, pltpu.roll(left, LANES - groups - 1, 1), 0.0)
    grads = grads + jnp.where(mine_lane == groups - 1, pltpu.roll(right, LANES - 1, 1), 0.0)
    packet = jnp.zeros((8, LANES), f32)
    for g in range(groups):
        packet = jnp.where(lane128 == 4 * groups + g, cells[g].astype(f32), packet)
    for q in range(depth // 8):
        block = grads[8 * q : 8 * q + 8]
        packet = packet + (pltpu.roll(block, groups * q, 1) if q else block)
    shift = groups * lax.rem(t, per)
    packet = pltpu.roll(packet, shift, 1)
    mine[...] = packet
    packets[t] = packet

    def track_copy(k, src, into, send, recv, sender):
        return pltpu.make_async_remote_copy(
            src,
            into.at[sender],
            send.at[k],
            recv.at[k],
            device_id=(d, lax.rem(t + k, ntr)),
            device_id_type=MESH,
        )

    def sent(k, src, into, send, recv):
        return track_copy(k, src, into, send, recv, t)

    def arrived(k, src, into, send, recv):
        return track_copy(k, src, into, send, recv, lax.rem(t + ntr - k, ntr))

    first = (mine, packets, send_p, recv_p)
    second = (below_mine, belows, send_q, recv_q)

    @pl.loop(1, ntr)
    def _(k):
        sent(k, *first).start()

    for copy in near:
        copy.wait()
    below = jnp.where(lane128 < groups, jnp.broadcast_to(near_total(near_c, 0, False), (8, LANES)), 0.0)
    below = pltpu.roll(below, shift, 1)
    below_mine[...] = below
    belows[t] = below

    @pl.loop(1, ntr)
    def _(k):
        sent(k, *second).start()

    focused[...] = jnp.where(inner, fint[...], joined3(nn(split3(edge), edge_of[...])))

    @pl.loop(1, ntr)
    def _(k):
        arrived(k, *first).wait_recv()

    chunk = lax.div(lane128, groups)
    for col in range(ntr // per):
        parts = []
        for q in range(depth // 8 + 1):
            acc = jnp.zeros((8, LANES), f32)
            for j in range(per):
                acc = jnp.where(chunk == (q + j) % per, packets[col * per + j], acc)
            parts.append(pltpu.roll(acc, LANES - groups * q, 1) if q else acc)
        lanes = pl.ds(col * LANES, LANES)
        g = jnp.concatenate(parts[:-1], axis=0)
        high = g.astype(bf16)
        ghigh[:, lanes] = high
        glow[:, lanes] = (g - high.astype(f32)).astype(bf16)
        cell = parts[-1][0:1]
        block = jnp.floor(cell * (1.0 / WIDE))
        block_of[:, lanes] = jnp.broadcast_to(block, (depth, LANES)).astype(bf16)
        place_of[:, lanes] = one_hot(iota((WIDE, LANES), 0).astype(f32) == cell - block * WIDE)

    nblock = grad.shape[1] // WIDE

    @pl.loop(0, nblock // PER_STEP)
    def _(step):
        highs = []
        lows = []
        for j in range(PER_STEP):
            mask = block_of[...] == (step * PER_STEP + j).astype(bf16)
            highs.append(jnp.where(mask, ghigh[...], jnp.zeros((), bf16)))
            lows.append(jnp.where(mask, glow[...], jnp.zeros((), bf16)))
        out = nt(jnp.concatenate(highs, axis=0), place_of[...]) + nt(jnp.concatenate(lows, axis=0), place_of[...])
        out = jnp.concatenate([out[depth * j : depth * (j + 1)] for j in range(PER_STEP)], axis=1)
        wide = PER_STEP * WIDE
        grad[:, pl.ds(pl.multiple_of(step * wide, wide), wide)] = out

    @pl.loop(1, ntr)
    def _(k):
        arrived(k, *second).wait_recv()

    cols = []
    for col in range(ntr // per):
        acc = belows[col * per, 0:1, :]
        for j in range(1, per):
            acc = acc + belows[col * per + j, 0:1, :]
        cols.append(acc)
    below = jnp.broadcast_to(jnp.concatenate(cols, axis=1), (nblock, ntr * groups))
    blocks = jnp.broadcast_to(block_of[...].astype(f32)[0:1], (nblock, ntr * groups))
    spread_below = jnp.where(blocks == iota((nblock, ntr * groups), 0).astype(f32), below, 0.0)
    rows_of[...] = joined3(nt(split3(spread_below), place_of[...]))

    @pl.loop(0, nblock, unroll=8)
    def _(j):
        lanes = pl.ds(pl.multiple_of(j * WIDE, WIDE), WIDE)
        grad[:, lanes] = grad[:, lanes] + jnp.broadcast_to(rows_of[pl.ds(j, 1), :], (depth, WIDE))

    @pl.loop(1, ntr)
    def _(k):
        sent(k, *first).wait_send()
        sent(k, *second).wait_send()


UNROLL = 2


def on_device(nd, ntr, slowness_cells, cell_of_group, taper, secant, primary, quadrature, observed):
    depth, traces, angles = primary.shape
    taps = taper.shape[1]
    ncell = slowness_cells.shape[1]
    groups = cell_of_group.shape[0]
    nedge = groups * 8
    total = ntr * groups
    nchunk = 8
    vmem = pl.BlockSpec(memory_space=pltpu.VMEM)
    anywhere = pl.BlockSpec(memory_space=pl.ANY)
    near = nd - 1
    side = 2 * nd
    dma = pltpu.SemaphoreType.DMA
    V = pltpu.VMEM
    slow = slowness_cells.reshape(depth // 8, 8, ncell // LANES, LANES).transpose(0, 2, 1, 3)
    gradient, image = pl.pallas_call(
        functools.partial(main_kernel, nd, ntr, nchunk),
        out_shape=(
            jax.ShapeDtypeStruct((depth, ncell), f32),
            jax.ShapeDtypeStruct((depth, traces), f32),
        ),
        in_specs=[anywhere] * 7,
        out_specs=(vmem, vmem),
        scratch_shapes=[
            pltpu.SMEM((groups,), jnp.int32),
            V((taps, angles), f32),
            V((1, angles), f32),
            V((depth, traces), f32),
            V(slow.shape, f32),
            V((depth, traces, angles), bf16),
            V((depth, traces, angles), bf16),
            V((3, 8, angles), f32),
            V((depth, LANES), f32),
            V((depth, 24, LANES), f32),
            V((depth, traces), f32),
            V((depth, traces), f32),
        ]
        + [V((depth, nedge), f32)] * 6
        + [
            V((nedge, traces), bf16),
            V((traces, LANES), bf16),
            V((nedge, LANES), bf16),
            V((nedge, LANES), bf16),
            V((depth, LANES), f32),
            V((near, 8, LANES), f32),
            V((2, depth, LANES), f32),
            V((side - 2, 8, LANES), f32),
            V((depth, LANES), f32),
            V((2, depth, LANES), f32),
            V((side - 2, 8, LANES), f32),
            V((depth, LANES), f32),
            V((near, 8, LANES), f32),
            V((8, LANES), f32),
            V((ntr, 8, LANES), f32),
            V((8, LANES), f32),
            V((ntr, 8, LANES), f32),
            V((depth, total), bf16),
            V((depth, total), bf16),
            V((depth, total), bf16),
            V((WIDE, total), bf16),
            V((ncell // WIDE, WIDE), f32),
            dma((4,)),
            dma,
            dma((nchunk,)),
            dma((nchunk,)),
            dma((near,)),
            dma((near,)),
            dma((side,)),
            dma((side,)),
            dma((side,)),
            dma((side,)),
            dma((near,)),
            dma((near,)),
            dma((ntr,)),
            dma((ntr,)),
            dma((ntr,)),
            dma((ntr,)),
        ],
        compiler_params=pltpu.CompilerParams(
            collective_id=0, has_side_effects=True, vmem_limit_bytes=VMEM_LIMIT
        ),
        name="radargram",
    )(slow, cell_of_group, taper.T, secant.reshape(1, angles), primary, quadrature, observed)
    return image, gradient


VMEM_LIMIT = 63 * 1024 * 1024


def solution(mesh):
    in_specs = (
        P("depth", None),
        P("track"),
        P(),
        P(),
        P("depth", "track", None),
        P("depth", "track", None),
        P("depth", "track"),
    )
    out_specs = (P("depth", "track"), P("depth", None))
    nd = mesh.shape["depth"]
    ntr = mesh.shape["track"]
    return jax.shard_map(
        functools.partial(on_device, nd, ntr), mesh=mesh, in_specs=in_specs, out_specs=out_specs, check_vma=False
    )
```

time: 47.3 us -> 41.7 us (0.88)
  Pallas kernels: 45 us -> 36.3 us
  local copies, waits for them, and re-layouts: 1.48 us -> 4.52 us
    pallas_call x1 -> x0, Pallas kernels: 5.59 us -> none  [on_device(): pl.pallas_call(functools.partial(scatter_kernel, groups), out_shape=(jax....]
    pallas_call x1, Pallas kernels: 39.4 us -> 36.3 us  [on_device(): pl.pallas_call(functools.partial(main_kernel, nd, ntr, nchunk), out_shape...]
    unnamed x1 -> x2, local copies, waits for them, and re-layouts: 1.48 us -> 4.52 us
where the time goes in v2:
time: 41.7 us; the launch traced here: 41.4 us
  Pallas kernels  36.3 us (87%)
  local copies, waits for them, and re-layouts  4.52 us (11%)
  between operations  0.64 us (2%)
    pallas_call x1, Pallas kernels, on_device(): pl.pallas_call(functools.partial(main_kernel, nd, ntr, nchunk), out_shape...  36.3 us
    unnamed x2, local copies, waits for them, and re-layouts  4.52 us

profile of v2, /device:TPU:1, one launch (start us, length us, event | category | flops | bytes accessed | tf_op | source)
XLA Modules:
  0.0 41.4 jit_solution(4756317704288411846)
XLA Ops:
  0.6 36.3 %radargram.1 = (f32[32,16384]{1,0:T(8,128)}, f32[32,512]{1,0:T(8,128)}) custom-call(f32[4,128,8,128]{3,2,1,0:T(8,128)} %bitcast.5, s32[16]{0:T(128)} %cells_hbm.1, f32[9,256]{1,0:T(8,128)} %bitcast.6, f32[1,256]{1,0:T(1,128)} %bitcast.7, bf16[32,512,256]{2,1,0:T(8,128)(2,1)} %prim_hbm.1, bf16[32,512,256]{2,1,0:T(8,128)(2,1)} %quad_hbm.1, f32[32,512]{1,0:T(8,128)} %seen_hbm.1), custom_call_target="tpu_custom_call" | custom-call | tf_op jit(solution)/shard_map/radargram/pallas_call | solution.py:571
  36.9 1.5 %copy.11 = f32[32,512]{1,0:T(8,128)} copy(f32[32,512]{1,0:T(8,128)} %get-tuple-element.8) | data formatting | bytes 131072
  38.4 3.0 %copy.12 = f32[32,16384]{1,0:T(8,128)} copy(f32[32,16384]{1,0:T(8,128)} %get-tuple-element.9) | data formatting | bytes 4194304

commit v3 on v2

--- a/solution.py
+++ b/solution.py
@@ -635,11 +635,39 @@
             collective_id=0, has_side_effects=True, vmem_limit_bytes=VMEM_LIMIT
         ),
         name="radargram",
-    )(slow, cell_of_group, taper.T, secant.reshape(1, angles), primary, quadrature, observed)
+    )(
+        *[
+            pltpu.with_memory_space_constraint(v, pltpu.HBM)
+            for v in (slow, cell_of_group, taper.T, secant.reshape(1, angles), primary, quadrature, observed)
+        ]
+    )
+    gradient, image = pl.pallas_call(
+        hand_out,
+        out_shape=(
+            jax.ShapeDtypeStruct((depth, ncell), f32),
+            jax.ShapeDtypeStruct((depth, traces), f32),
+        ),
+        in_specs=[anywhere] * 2,
+        out_specs=(anywhere, anywhere),
+        scratch_shapes=[dma((2,))],
+        compiler_params=pltpu.CompilerParams(vmem_limit_bytes=1024 * 1024),
+        name="hand_out",
+    )(gradient, image)
     return image, gradient
 
 
-VMEM_LIMIT = 63 * 1024 * 1024
+def hand_out(grad, image, grad_out, image_out, sems):
+    copies = [
+        pltpu.make_async_copy(grad, grad_out, sems.at[0]),
+        pltpu.make_async_copy(image, image_out, sems.at[1]),
+    ]
+    for copy in copies:
+        copy.start()
+    for copy in copies:
+        copy.wait()
+
+
+VMEM_LIMIT = 40 * 1024 * 1024
 
 
 def solution(mesh):

time: 41.7 us -> 37 us (0.89)
  local copies, waits for them, and re-layouts: 4.52 us -> 0 us
    unnamed x2 -> x0, local copies, waits for them, and re-layouts: 4.52 us -> none
    pallas_call x1, Pallas kernels: 36.3 us -> 34.9 us  [on_device(): pl.pallas_call(functools.partial(main_kernel, nd, ntr, nchunk), out_shape...]
    pallas_call x0 -> x1, Pallas kernels: none -> 1.34 us  [on_device(): pl.pallas_call(hand_out, out_shape=(jax.ShapeDtypeStruct((depth, ncell),...]
where the time goes in v3:
time: 37 us; the launch traced here: 36.9 us
  Pallas kernels  36.2 us (98%)
  between operations  0.64 us (2%)
    pallas_call x1, Pallas kernels, on_device(): pl.pallas_call(functools.partial(main_kernel, nd, ntr, nchunk), out_shape...  34.9 us
    pallas_call x1, Pallas kernels, on_device(): pl.pallas_call(hand_out, out_shape=(jax.ShapeDtypeStruct((depth, ncell),...  1.34 us

profile of v3, /device:TPU:1, one launch (start us, length us, event | category | flops | bytes accessed | tf_op | source)
XLA Modules:
  0.0 36.9 jit_solution(7031415743592209724)
XLA Ops:
  0.6 34.9 %radargram.1 = (f32[32,16384]{1,0:T(8,128)S(1)}, f32[32,512]{1,0:T(8,128)S(1)}) custom-call(f32[4,128,8,128]{3,2,1,0:T(8,128)} %bitcast.5, s32[16]{0:T(128)} %cells_hbm.1, f32[9,256]{1,0:T(8,128)} %bitcast.6, f32[1,256]{1,0:T(1,128)} %bitcast.7, bf16[32,512,256]{2,1,0:T(8,128)(2,1)} %prim_hbm.1, bf16[32,512,256]{2,1,0:T(8,128)(2,1)} %quad_hbm.1, ...), custom_call_target="tpu_custom_call" | custom-call | tf_op jit(solution)/shard_map/radargram/pallas_call | solution.py:571
  35.5 1.3 %hand_out.1 = (f32[32,16384]{1,0:T(8,128)}, f32[32,512]{1,0:T(8,128)}) custom-call(f32[32,16384]{1,0:T(8,128)S(1)} %get-tuple-element.6.grad, f32[32,512]{1,0:T(8,128)S(1)} %get-tuple-element.7.image), custom_call_target="tpu_custom_call" | custom-call | tf_op jit(solution)/shard_map/hand_out/pallas_call | solution.py:644

commit v4 on v3

--- a/solution.py
+++ b/solution.py
@@ -73,9 +73,9 @@
     return [
         pltpu.make_async_remote_copy(
             src.at[pl.ds(tile, 8)],
-            into.at[k - 1],
-            send.at[k - 1],
-            recv.at[k - 1],
+            into.at[pl.ds(8 * (k - 1), 8)],
+            send,
+            recv,
             device_id=peer_of(k, 0, nd, nt_),
             device_id_type=MESH,
         )
@@ -83,23 +83,27 @@
     ]
 
 
-def side_copies(nd, nt_, src, tile, wide, narrow, send, recv):
+def side_copies(nd, nt_, src, tile, into, send, recv):
+    depth = src.shape[0]
     copies = []
     for i, o in enumerate((1, -1)):
         copies.append(
             pltpu.make_async_remote_copy(
-                src, wide.at[i], send.at[i], recv.at[i], device_id=peer_of(0, o, nd, nt_), device_id_type=MESH
+                src,
+                into.at[pl.ds(i * depth, depth)],
+                send,
+                recv,
+                device_id=peer_of(0, o, nd, nt_),
+                device_id_type=MESH,
             )
         )
-    for k in range(1, nd):
-        for i, o in enumerate((1, -1)):
-            at = 2 * (k - 1) + i
+        for k in range(1, nd):
             copies.append(
                 pltpu.make_async_remote_copy(
                     src.at[pl.ds(tile, 8)],
-                    narrow.at[at],
-                    send.at[2 + at],
-                    recv.at[2 + at],
+                    into.at[pl.ds(2 * depth + 8 * (2 * (k - 1) + i), 8)],
+                    send,
+                    recv,
                     device_id=peer_of(k, o, nd, nt_),
                     device_id_type=MESH,
                 )
@@ -107,8 +111,16 @@
     return copies
 
 
+def wait_all(into, send, recv, nd, nt_):
+    copy = pltpu.make_async_remote_copy(
+        into, into, send, recv, device_id=peer_of(1, 0, nd, nt_), device_id_type=MESH
+    )
+    copy.wait_recv()
+    copy.wait_send()
+
+
 WIDE = 256
-PER_STEP = 8
+PER_STEP = 16
 
 
 def main_kernel(
@@ -148,13 +160,13 @@
     to_hi,
     halo_a,
     near_a,
-    wide_a,
-    narrow_a,
+    side_a,
     halo_b,
-    wide_b,
-    narrow_b,
+    side_b,
     halo_c,
     near_c,
+    cells_mine,
+    cell_rows,
     mine,
     packets,
     below_mine,
@@ -172,6 +184,8 @@
     recv_a,
     send_as,
     recv_as,
+    send_cells,
+    recv_cells,
     send_b,
     recv_b,
     send_c,
@@ -239,10 +253,41 @@
     halo_a[...] = own
 
     pl.semaphore_wait(barrier, ntr - 1 + 3 * (nd - 1))
-    near = near_copies(nd, ntr, halo_a, depth - 8, near_a, send_a, recv_a)
-    side_a = side_copies(nd, ntr, halo_a, depth - 8, wide_a, narrow_a, send_as, recv_as)
-    for copy in near + side_a:
+    for copy in near_copies(nd, ntr, halo_a, depth - 8, near_a, send_a, recv_a):
         copy.start()
+    for copy in side_copies(nd, ntr, halo_a, depth - 8, side_a, send_as, recv_as):
+        copy.start()
+
+    lane1 = iota((1, LANES), 1)
+    shift = groups * lax.rem(t, per)
+    row = jnp.zeros((1, LANES), f32)
+    for g in range(groups):
+        row = jnp.where(lane1 == shift + g, cells[g].astype(f32), row)
+    cells_mine[...] = row
+    cell_rows[t] = row
+
+    def to_track(k, src, into, send, recv):
+        pltpu.make_async_remote_copy(
+            src,
+            into.at[t],
+            send,
+            recv,
+            device_id=(d, lax.rem(t + k, ntr)),
+            device_id_type=MESH,
+        ).start()
+
+    @pl.loop(1, ntr)
+    def _(k):
+        to_track(k, cells_mine, cell_rows, send_cells, recv_cells)
+
+    def others(ref):
+        return ref.at[pl.ds(0, ntr - 1)]
+
+    def track_row(ref, col):
+        acc = ref[col * per]
+        for j in range(1, per):
+            acc = acc + ref[col * per + j]
+        return acc
 
     for copy in small[1:]:
         copy.wait()
@@ -275,20 +320,21 @@
     to_hi[...] = one_hot(jnp.where((bi > 0) | behind_row, bi, groups + 1) == el)
     seen_edge = joined3(nt(split3(seen[...]), edge_of[...]))
 
-    for copy in near:
-        copy.wait()
+    wait_all(near_a, send_a, recv_a, nd, ntr)
 
     def near_total(into, rowi, up):
         acc = jnp.zeros((1, LANES), f32)
         for k in range(1, nd):
-            acc = acc + jnp.where((k <= d) if up else (k > d), into[k - 1, rowi : rowi + 1, :], 0.0)
+            at = 8 * (k - 1) + rowi
+            acc = acc + jnp.where((k <= d) if up else (k > d), into[at : at + 1, :], 0.0)
         return acc
 
-    def side_total(i, rowi, narrow, up):
-        acc = jnp.zeros((1, LANES), f32)
+    def side_total(i, rowi, into, up):
+        acc = into[i * depth : (i + 1) * depth, :]
         for k in range(1, nd):
             use = (k <= d) if up else (k > d)
-            acc = acc + jnp.where(use, narrow[2 * (k - 1) + i, rowi : rowi + 1, :], 0.0)
+            at = 2 * depth + 8 * (2 * (k - 1) + i) + rowi
+            acc = acc + jnp.where(use, into[at : at + 1, :], 0.0)
         return acc
 
     turn = 1.0 / (2.0 * math.pi)
@@ -371,7 +417,7 @@
             picked = jnp.where(place & (lane128 < 8), v, 0.0)
             ref[pl.ds(z, 1), :] = jnp.sum(picked, axis=0, keepdims=True)
 
-    @pl.loop(0, nchunk // 2)
+    @pl.loop(0, FIRST_CHUNKS)
     def _(i):
         for copy in chunk_copies(i):
             copy.wait()
@@ -380,14 +426,14 @@
         def _(j):
             each_depth(i * zc + j)
 
-    for i in range(nchunk // 2, nchunk):
+    @pl.loop(FIRST_CHUNKS, nchunk)
+    def _(i):
         for copy in chunk_copies(i):
             copy.wait()
 
-    for copy in side_a:
-        copy.wait()
-    left = jnp.where(t > 0, wide_a[0] + side_total(0, 7, narrow_a, True), 0.0) * turn
-    right = jnp.where(t < ntr - 1, wide_a[1] + side_total(1, 7, narrow_a, True), 0.0) * turn
+    wait_all(side_a, send_as, recv_as, nd, ntr)
+    left = jnp.where(t > 0, side_total(0, 7, side_a, True), 0.0) * turn
+    right = jnp.where(t < ntr - 1, side_total(1, 7, side_a, True), 0.0) * turn
     outer = jnp.where(mine_lane == groups, pltpu.roll(left, 1, 1), 0.0)
     line[...] = jnp.where(mine_lane == groups + 1, pltpu.roll(right, groups + 1, 1), outer)
     spread_rows(groups, 8)
@@ -411,11 +457,18 @@
     halo_b[...] = suffix(
         jnp.where(mine_lane == groups, to_left, jnp.where(mine_lane == groups + 1, to_right, 0.0))
     )
-    side_b = side_copies(nd, ntr, halo_b, 0, wide_b, narrow_b, send_b, recv_b)
-    for copy in side_b:
+    for copy in side_copies(nd, ntr, halo_b, 0, side_b, send_b, recv_b):
         copy.start()
 
-    @pl.loop(depth // 2, depth, unroll=UNROLL)
+    wait_all(others(cell_rows), send_cells, recv_cells, nd, ntr)
+    for col in range(ntr // per):
+        lanes = pl.ds(col * LANES, LANES)
+        cell = track_row(cell_rows, col)
+        block = jnp.floor(cell * (1.0 / WIDE))
+        block_of[:, lanes] = jnp.broadcast_to(block, (depth, LANES)).astype(bf16)
+        place_of[:, lanes] = one_hot(iota((WIDE, LANES), 0).astype(f32) == cell - block * WIDE)
+
+    @pl.loop(FIRST_CHUNKS * zc, depth, unroll=UNROLL)
     def _(z):
         each_depth(z)
 
@@ -429,85 +482,65 @@
     sums = sums + joined3(nn(split3(resid * (bhi[...] + hiside[...])), to_hi[...]))
     sums = suffix(sums)
     halo_c[...] = sums
-    near = near_copies(nd, ntr, halo_c, 0, near_c, send_c, recv_c)
-    for copy in near:
+    for copy in near_copies(nd, ntr, halo_c, 0, near_c, send_c, recv_c):
         copy.start()
 
-    for copy in side_b:
-        copy.wait()
-    left = jnp.where(t > 0, wide_b[0] + side_total(0, 0, narrow_b, False), 0.0)
-    right = jnp.where(t < ntr - 1, wide_b[1] + side_total(1, 0, narrow_b, False), 0.0)
+    wait_all(side_b, send_b, recv_b, nd, ntr)
+    left = jnp.where(t > 0, side_total(0, 0, side_b, False), 0.0)
+    right = jnp.where(t < ntr - 1, side_total(1, 0, side_b, False), 0.0)
     grads = jnp.where(mine_lane < groups, sums, 0.0)
     grads = grads + jnp.where(mine_lane == 0, pltpu.roll(left, LANES - groups - 1, 1), 0.0)
     grads = grads + jnp.where(mine_lane == groups - 1, pltpu.roll(right, LANES - 1, 1), 0.0)
     packet = jnp.zeros((8, LANES), f32)
-    for g in range(groups):
-        packet = jnp.where(lane128 == 4 * groups + g, cells[g].astype(f32), packet)
     for q in range(depth // 8):
         block = grads[8 * q : 8 * q + 8]
         packet = packet + (pltpu.roll(block, groups * q, 1) if q else block)
-    shift = groups * lax.rem(t, per)
-    packet = pltpu.roll(packet, shift, 1)
+    packet = packet + pltpu.roll(pltpu.roll(packet, 4, 0), LANES // 2, 1)
+    packet = pltpu.roll(packet, shift, 1)[0:4]
     mine[...] = packet
     packets[t] = packet
 
-    def track_copy(k, src, into, send, recv, sender):
-        return pltpu.make_async_remote_copy(
-            src,
-            into.at[sender],
-            send.at[k],
-            recv.at[k],
-            device_id=(d, lax.rem(t + k, ntr)),
-            device_id_type=MESH,
-        )
-
-    def sent(k, src, into, send, recv):
-        return track_copy(k, src, into, send, recv, t)
-
-    def arrived(k, src, into, send, recv):
-        return track_copy(k, src, into, send, recv, lax.rem(t + ntr - k, ntr))
-
-    first = (mine, packets, send_p, recv_p)
-    second = (below_mine, belows, send_q, recv_q)
-
     @pl.loop(1, ntr)
     def _(k):
-        sent(k, *first).start()
-
-    for copy in near:
-        copy.wait()
-    below = jnp.where(lane128 < groups, jnp.broadcast_to(near_total(near_c, 0, False), (8, LANES)), 0.0)
-    below = pltpu.roll(below, shift, 1)
+        to_track(k, mine, packets, send_p, recv_p)
+
+    wait_all(near_c, send_c, recv_c, nd, ntr)
+    below = pltpu.roll(
+        jnp.broadcast_to(jnp.where(lane1 < groups, near_total(near_c, 0, False), 0.0), (8, LANES)), shift, 1
+    )[0:1]
     below_mine[...] = below
     belows[t] = below
 
     @pl.loop(1, ntr)
     def _(k):
-        sent(k, *second).start()
+        to_track(k, below_mine, belows, send_q, recv_q)
 
     focused[...] = jnp.where(inner, fint[...], joined3(nn(split3(edge), edge_of[...])))
-
-    @pl.loop(1, ntr)
-    def _(k):
-        arrived(k, *first).wait_recv()
-
-    chunk = lax.div(lane128, groups)
+    wait_all(others(packets), send_p, recv_p, nd, ntr)
+
+    chunk = lax.div(iota((4, LANES), 1), groups)
     for col in range(ntr // per):
         parts = []
-        for q in range(depth // 8 + 1):
-            acc = jnp.zeros((8, LANES), f32)
+        for c in range(per):
+            acc = jnp.zeros((4, LANES), f32)
             for j in range(per):
-                acc = jnp.where(chunk == (q + j) % per, packets[col * per + j], acc)
-            parts.append(pltpu.roll(acc, LANES - groups * q, 1) if q else acc)
+                acc = jnp.where(chunk == (c + j) % per, packets[col * per + j], acc)
+            parts.append(acc)
         lanes = pl.ds(col * LANES, LANES)
-        g = jnp.concatenate(parts[:-1], axis=0)
+        nq = depth // 8
+        pieces = []
+        for q in range(nq):
+            for h in range(2):
+                c = q + nq * h
+                both = jnp.concatenate([parts[c], parts[c]], axis=0)
+                pieces.append(pltpu.roll(both, LANES - groups * c, 1) if c else both)
+        low_rows = iota((8, LANES), 0) < 4
+        g = jnp.concatenate(
+            [jnp.where(low_rows, pieces[2 * q], pieces[2 * q + 1]) for q in range(nq)], axis=0
+        )
         high = g.astype(bf16)
         ghigh[:, lanes] = high
         glow[:, lanes] = (g - high.astype(f32)).astype(bf16)
-        cell = parts[-1][0:1]
-        block = jnp.floor(cell * (1.0 / WIDE))
-        block_of[:, lanes] = jnp.broadcast_to(block, (depth, LANES)).astype(bf16)
-        place_of[:, lanes] = one_hot(iota((WIDE, LANES), 0).astype(f32) == cell - block * WIDE)
 
     nblock = grad.shape[1] // WIDE
 
@@ -524,17 +557,9 @@
         wide = PER_STEP * WIDE
         grad[:, pl.ds(pl.multiple_of(step * wide, wide), wide)] = out
 
-    @pl.loop(1, ntr)
-    def _(k):
-        arrived(k, *second).wait_recv()
-
-    cols = []
-    for col in range(ntr // per):
-        acc = belows[col * per, 0:1, :]
-        for j in range(1, per):
-            acc = acc + belows[col * per + j, 0:1, :]
-        cols.append(acc)
-    below = jnp.broadcast_to(jnp.concatenate(cols, axis=1), (nblock, ntr * groups))
+    wait_all(others(belows), send_q, recv_q, nd, ntr)
+    below = jnp.concatenate([track_row(belows, col) for col in range(ntr // per)], axis=1)
+    below = jnp.broadcast_to(below, (nblock, ntr * groups))
     blocks = jnp.broadcast_to(block_of[...].astype(f32)[0:1], (nblock, ntr * groups))
     spread_below = jnp.where(blocks == iota((nblock, ntr * groups), 0).astype(f32), below, 0.0)
     rows_of[...] = joined3(nt(split3(spread_below), place_of[...]))
@@ -544,12 +569,8 @@
         lanes = pl.ds(pl.multiple_of(j * WIDE, WIDE), WIDE)
         grad[:, lanes] = grad[:, lanes] + jnp.broadcast_to(rows_of[pl.ds(j, 1), :], (depth, WIDE))
 
-    @pl.loop(1, ntr)
-    def _(k):
-        sent(k, *first).wait_send()
-        sent(k, *second).wait_send()
-
-
+
+FIRST_CHUNKS = 2
 UNROLL = 2
 
 
@@ -564,7 +585,6 @@
     vmem = pl.BlockSpec(memory_space=pltpu.VMEM)
     anywhere = pl.BlockSpec(memory_space=pl.ANY)
     near = nd - 1
-    side = 2 * nd
     dma = pltpu.SemaphoreType.DMA
     V = pltpu.VMEM
     slow = slowness_cells.reshape(depth // 8, 8, ncell // LANES, LANES).transpose(0, 2, 1, 3)
@@ -597,18 +617,18 @@
             V((nedge, LANES), bf16),
             V((nedge, LANES), bf16),
             V((depth, LANES), f32),
-            V((near, 8, LANES), f32),
-            V((2, depth, LANES), f32),
-            V((side - 2, 8, LANES), f32),
+            V((8 * near, LANES), f32),
+            V((2 * depth + 16 * near, LANES), f32),
             V((depth, LANES), f32),
-            V((2, depth, LANES), f32),
-            V((side - 2, 8, LANES), f32),
+            V((2 * depth + 16 * near, LANES), f32),
             V((depth, LANES), f32),
-            V((near, 8, LANES), f32),
-            V((8, LANES), f32),
-            V((ntr, 8, LANES), f32),
-            V((8, LANES), f32),
-            V((ntr, 8, LANES), f32),
+            V((8 * near, LANES), f32),
+            V((1, LANES), f32),
+            V((ntr, 1, LANES), f32),
+            V((4, LANES), f32),
+            V((ntr, 4, LANES), f32),
+            V((1, LANES), f32),
+            V((ntr, 1, LANES), f32),
             V((depth, total), bf16),
             V((depth, total), bf16),
             V((depth, total), bf16),
@@ -618,19 +638,8 @@
             dma,
             dma((nchunk,)),
             dma((nchunk,)),
-            dma((near,)),
-            dma((near,)),
-            dma((side,)),
-            dma((side,)),
-            dma((side,)),
-            dma((side,)),
-            dma((near,)),
-            dma((near,)),
-            dma((ntr,)),
-            dma((ntr,)),
-            dma((ntr,)),
-            dma((ntr,)),
-        ],
+        ]
+        + [dma] * 14,
         compiler_params=pltpu.CompilerParams(
             collective_id=0, has_side_effects=True, vmem_limit_bytes=VMEM_LIMIT
         ),

time: 37 us -> 34.2 us (0.924)
  Pallas kernels: 36.2 us -> 33.4 us
    pallas_call x1, Pallas kernels: 34.9 us -> 32 us  [on_device(): pl.pallas_call(functools.partial(main_kernel, nd, ntr, nchunk), out_shape...]
where the time goes in v4:
time: 34.2 us; the launch traced here: 34 us
  Pallas kernels  33.4 us (98%)
  between operations  0.64 us (2%)
    pallas_call x1, Pallas kernels, on_device(): pl.pallas_call(functools.partial(main_kernel, nd, ntr, nchunk), out_shape...  32 us
    pallas_call x1, Pallas kernels, on_device(): pl.pallas_call(hand_out, out_shape=(jax.ShapeDtypeStruct((depth, ncell),...  1.34 us

profile of v4, /device:TPU:1, one launch (start us, length us, event | category | flops | bytes accessed | tf_op | source)
XLA Modules:
  0.0 34.0 jit_solution(13954816856832428542)
XLA Ops:
  0.6 32.0 %radargram.1 = (f32[32,16384]{1,0:T(8,128)S(1)}, f32[32,512]{1,0:T(8,128)S(1)}) custom-call(f32[4,128,8,128]{3,2,1,0:T(8,128)} %bitcast.5, s32[16]{0:T(128)} %cells_hbm.1, f32[9,256]{1,0:T(8,128)} %bitcast.6, f32[1,256]{1,0:T(1,128)} %bitcast.7, bf16[32,512,256]{2,1,0:T(8,128)(2,1)} %prim_hbm.1, bf16[32,512,256]{2,1,0:T(8,128)(2,1)} %quad_hbm.1, ...), custom_call_target="tpu_custom_call" | custom-call | tf_op jit(solution)/shard_map/radargram/pallas_call | solution.py:591
  32.7 1.3 %hand_out.1 = (f32[32,16384]{1,0:T(8,128)}, f32[32,512]{1,0:T(8,128)}) custom-call(f32[32,16384]{1,0:T(8,128)S(1)} %get-tuple-element.6.grad, f32[32,512]{1,0:T(8,128)S(1)} %get-tuple-element.7.image), custom_call_target="tpu_custom_call" | custom-call | tf_op jit(solution)/shard_map/hand_out/pallas_call | solution.py:653
